TPU v7x, 32 devices: a whole 2x2x4 slice. The times are simulated.
32 devices in a mesh: seq: 4 (over x, core), ctx: 4 (over z), head: 2 (over y).
Axes of the slice: x: 2, y: 2, z: 4, core: 2. Of those that a mesh axis runs over, the one named last changes fastest.
Arguments:
- stream: bfloat16 [4, 256, 2880], P('seq', 'ctx'), may hold values from -6 to 6
- query_weight: bfloat16 [2880, 4096], P(None, 'head'), may hold values from -0.109375 to 0.109375
- cache_keys: bfloat16 [4, 8192, 8, 64], P('seq', 'ctx', 'head'), may hold values from -1000 to 1000
- cache_values: bfloat16 [4, 8192, 8, 64], P('seq', 'ctx', 'head'), may hold values from -6 to 6
- new_keys: bfloat16 [4, 256, 8, 64], P('seq', 'ctx', 'head'), may hold values from -18 to 18
- new_values: bfloat16 [4, 256, 8, 64], P('seq', 'ctx', 'head'), may hold values from -6 to 6
- out_weight: bfloat16 [4096, 2880], P('head'), may hold values from -0.09375 to 0.09375
- norm_gain: float32 [2880], replicated, may hold values from 0.5 to 1.5
- expert_ids: int32 [4, 256, 4], P('seq', 'ctx'), may hold values from 0 to 15, all different within a row; in each aligned block of 64 rows (0 to 63, 64 to 127, ..., all dimensions but the last counted through in order) at most 16 rows name the same one
- expert_weights: float32 [4, 256, 4], P('seq', 'ctx'), may hold values from 0.1 to 1
- gate_weight: bfloat16 [16, 2880, 2880], P(('seq', 'ctx'), None, 'head'), may hold values from -0.109375 to 0.109375
- up_weight: bfloat16 [16, 2880, 2880], P(('seq', 'ctx'), None, 'head'), may hold values from -0.109375 to 0.109375
- down_weight: bfloat16 [16, 2880, 2880], P(('seq', 'ctx'), 'head'), may hold values from -0.109375 to 0.109375
Outputs:
- mixed: bfloat16 [4, 256, 2880], P('seq', 'ctx', 'head')
Inputs may be any that keep to these rules, and one draw needn't show every extreme that they name: `expert_ids`: in each aligned block of 64 rows (the tokens of one device) no expert is named by more than 16 rows; each row names 4 different experts.
All inputs are finite; a program needn't handle non-finite values.
Results may differ from a plain program's by a relative error of at most 0.015.
Values may be sent and summed in bfloat16 or wider, within the bound.
No kernel may reach another device: no remote copies, remote signals or barrier semaphores. Data moves between devices by JAX's collectives and lax.ppermute only.
A program may use at most 128 MiB of HBM per device.

v0:
```python
import math

import jax
import jax.numpy as jnp
from jax import lax
from jax.sharding import PartitionSpec as P

CAP = 16


def passed_along(block, axis, distance):
    devices = range(lax.axis_size(axis))
    route = [((i - distance) % len(devices), i) for i in devices]
    return lax.ppermute(block, axis, route)


def body(
    stream,
    query_weight,
    cache_keys,
    cache_values,
    new_keys,
    new_values,
    out_weight,
    norm_gain,
    expert_ids,
    expert_weights,
    gate_weight,
    up_weight,
    down_weight,
):
    tokens = stream[0]
    count = tokens.shape[0]
    model = tokens.shape[1]
    kv_local = cache_keys.shape[2]
    head_dim = cache_keys.shape[3]
    group = query_weight.shape[1] // (kv_local * head_dim)
    cache_len = cache_keys.shape[1]
    height = count * group
    cycles = lax.axis_size("ctx")
    place = lax.axis_index("ctx")
    scale = 1.0 / math.sqrt(head_dim)
    query = jnp.dot(tokens, query_weight, preferred_element_type=jnp.float32).astype(jnp.bfloat16)
    query = (
        query.reshape(count, kv_local, group, head_dim)
        .transpose(1, 0, 2, 3)
        .reshape(kv_local, height, head_dim)
    )
    keys = jnp.concatenate([cache_keys[0], new_keys[0]], axis=0).transpose(1, 0, 2)
    values = jnp.concatenate([cache_values[0], new_values[0]], axis=0).transpose(1, 0, 2)
    extent = keys.shape[1]
    key_index = lax.broadcasted_iota(jnp.int32, (height, extent), 1)
    tok_index = lax.broadcasted_iota(jnp.int32, (height, extent), 0) // group
    fresh = key_index - cache_len
    blank = (
        jnp.full((kv_local, height), -jnp.inf, jnp.float32),
        jnp.zeros((kv_local, height), jnp.float32),
        jnp.zeros((kv_local, height, head_dim), jnp.float32),
    )

    def absorb(block, state, sources):
        top, total, numerator = state
        anchor = sources[:, None]
        allowed = (
            (key_index < cache_len) | (place < anchor) | (place == anchor) & (fresh <= tok_index)
        )
        scores = jnp.einsum("hrd,hkd->hrk", block, keys, preferred_element_type=jnp.float32) * scale
        scores = jnp.where(allowed[None], scores, -jnp.inf)
        new_top = jnp.maximum(top, jnp.max(scores, axis=-1))
        weights = jnp.exp(scores - new_top[..., None])
        fade = jnp.exp(top - new_top)
        total = total * fade + jnp.sum(weights, axis=-1)
        numerator = numerator * fade[..., None] + jnp.einsum(
            "hrk,hkd->hrd", weights.astype(jnp.bfloat16), values, preferred_element_type=jnp.float32
        )
        return (new_top, total, numerator)

    def turn(step, carry):
        sources = jnp.full((height,), (place - step) % cycles, jnp.int32)
        state = absorb(carry[0].astype(jnp.bfloat16), carry[1:], sources)
        return passed_along((carry[0],) + state, "ctx", 1)

    final = lax.fori_loop(0, cycles, turn, (query.astype(jnp.float32),) + blank)
    top, total, numerator = (final[1], final[2], final[3])
    attn = (numerator / total[..., None]).astype(jnp.bfloat16)
    attn = (
        attn.reshape(kv_local, count, group, head_dim)
        .transpose(1, 0, 2, 3)
        .reshape(count, kv_local * group * head_dim)
    )
    projected = jnp.dot(attn, out_weight, preferred_element_type=jnp.float32)
    width = model // lax.axis_size("head")
    offset = lax.axis_index("head") * width
    resid = tokens.astype(jnp.float32) + lax.psum(projected.astype(jnp.bfloat16), "head").astype(
        jnp.float32
    )
    normed = (
        resid * lax.rsqrt(jnp.mean(resid * resid, axis=-1, keepdims=True) + 1e-05) * norm_gain
    ).astype(jnp.bfloat16)
    resid_own = lax.dynamic_slice_in_dim(resid, offset, width, 1)
    experts = lax.axis_size("seq") * lax.axis_size("ctx")
    slots = experts * CAP
    chosen = expert_ids[0].reshape(-1)
    onehot = (chosen[:, None] == lax.broadcasted_iota(jnp.int32, (1, experts), 1)).astype(jnp.int32)
    before = jnp.cumsum(onehot, axis=0) - onehot
    target = chosen * CAP + jnp.sum(before * onehot, axis=1)
    matches = target[None, :] == lax.broadcasted_iota(jnp.int32, (slots, 1), 0)
    select = jnp.sum(matches.astype(jnp.float32).reshape(slots, count, -1), axis=-1).astype(
        jnp.bfloat16
    )
    packed = jnp.dot(select, normed, preferred_element_type=jnp.float32).astype(jnp.bfloat16)
    packed = packed.reshape(experts, CAP, normed.shape[1])
    arrived = lax.all_to_all(packed, ("seq", "ctx"), split_axis=0, concat_axis=0, tiled=True)
    rows = arrived.reshape(slots, normed.shape[1])
    gate = jnp.dot(rows, gate_weight[0], preferred_element_type=jnp.float32)
    up = jnp.dot(rows, up_weight[0], preferred_element_type=jnp.float32)
    hidden = (gate * jax.nn.sigmoid(1.702 * gate) * (up + 1.0)).astype(jnp.bfloat16)
    columns = down_weight[0]
    expert_out = lax.psum_scatter(
        jnp.einsum("fd,rf->dr", columns, hidden, preferred_element_type=jnp.float32).astype(
            jnp.bfloat16
        ),
        "head",
        scatter_dimension=0,
        tiled=True,
    )
    returned = lax.all_to_all(expert_out, ("seq", "ctx"), split_axis=1, concat_axis=1, tiled=True)
    spread_weights = jnp.where(matches.T, expert_weights[0].reshape(-1)[:, None], 0.0)
    spread_weights = jnp.sum(spread_weights.reshape(count, -1, slots), axis=1)
    moe = lax.dot_general(
        spread_weights,
        returned.astype(jnp.float32),
        (((1,), (1,)), ((), ())),
        precision=lax.Precision.HIGHEST,
    )
    return (resid_own + moe).astype(jnp.bfloat16)[None]


def solution(mesh):
    in_specs = (
        P("seq", "ctx", None),
        P(None, "head"),
        P("seq", "ctx", "head", None),
        P("seq", "ctx", "head", None),
        P("seq", "ctx", "head", None),
        P("seq", "ctx", "head", None),
        P("head", None),
        P(),
        P("seq", "ctx", None),
        P("seq", "ctx", None),
        P(("seq", "ctx"), None, "head"),
        P(("seq", "ctx"), None, "head"),
        P(("seq", "ctx"), "head", None),
    )
    out_specs = P("seq", "ctx", "head")
    return jax.shard_map(body, mesh=mesh, in_specs=in_specs, out_specs=out_specs, check_vma=False)
```

profile of v0, /device:TPU:0, one launch (start us, length us, event | category | flops | bytes accessed | tf_op | source)
XLA Modules:
  0.0 386.5 jit_solution(13312295736175083786)
XLA Ops:
  6.6 0.9 copy.34
  7.5 0.9 copy.35
  8.5 6.7 %fusion.43 = bf16[64,2048]{1,0:T(8,128)(2,1)S(1)} fusion(bf16[2880,2048]{1,0:T(8,128)(2,1)} %param.16, bf16[1,64,2880]{2,1,0:T(8,128)(2,1)} %param.15), kind=kOutput, calls=%fused_computation.38 | convolution fusion | flops 755105792 | bytes 12427264 | tf_op jit(solution)/shard_map/dot_general | solution.py:43
  16.4 2.4 maximum_bitcast_fusion
  18.9 205.2 %while.22 = (s32[]{:T(128)}, bf16[4,512,64]{1,2,0:T(8,128)(2,1)S(1)}, f32[4,512]{1,0:T(4,128)S(1)}, f32[4,512]{1,0:T(4,128)S(1)}, f32[4,512,64]{1,2,0:T(8,128)S(...) while((s32[]{:T(128)}, ...), condition=%wide.region_3.4_spmd.clone, body=%wide.region_0.3_spmd.clone.sunk | while | flops 1161629696 | bytes 63567040 | solution.py:83
  19.1 1.3 fusion.86
  20.5 7.7 %fusion.87 = (f32[4,512]{1,0:T(4,128)S(1)}, f32[4,512,2112]{1,2,0:T(8,128)}) fusion(pred[512,2112]{0,1:T(8,128)(4,1)S(1)} %fusion.86, bf16[4,512,64]{1,2,0:T(8,128)(2,1)S(1)} %copy.57, bf16[4,2112,64]{1,2,0:T(8,128)(2,1)S(1)} %get-tuple-element.480), kind=kOutput, calls=%fused_computation.4.clone.1 | convolution fusion | flops 566622208 | bytes 19734528 | tf_op jit(solution)/shard_map/while/body/eval_jaxpr/hrd,hkd->hrk/dot_general | solution.py:67
  28.2 9.6 %fusion.88 = f32[4,512]{1,0:T(4,128)S(1)} fusion(f32[4,512,2112]{1,2,0:T(8,128)} %get-tuple-element.439, f32[4,512]{1,0:T(4,128)S(1)} %max.12, pred[512,2112]{0,1:T(8,128)(4,1)S(1)} %fusion.86), kind=kLoop, calls=%fused_computation.6.clone.1 | loop fusion | flops 17299456 | bytes 18399232 | tf_op jit(solution)/shard_map/while/body/eval_jaxpr/reduce_sum | solution.py:72
  37.8 11.6 %fusion.89 = f32[4,512,64]{1,2,0:T(8,128)} fusion(bf16[4,2112,64]{1,2,0:T(8,128)(2,1)} %get-tuple-element.481, f32[4,512,2112]{1,2,0:T(8,128)} %get-tuple-element.439, f32[4,512]{1,0:T(4,128)S(1)} %max.12, pred[512,2112]{0,1:T(8,128)(4,1)S(1)} %fusion.86, f32[4,512,64]{1,2,0:T(8,128)S(1)} %get-tuple-element.462, f32[4,512]{1,0:T(4,128)S(1)} %get-tuple-element.441), kind=kOutput, calls=%fused_computation.15.clone.1 | convolution fusion | flops 571211776 | bytes 20529152 | tf_op jit(solution)/shard_map/while/body/eval_jaxpr/hrk,hkd->hrd/dot_general | solution.py:73
  49.4 3.1 collective-permute-start.3
  52.4 1.6 collective-permute-start
  54.0 1.6 collective-permute-start.1
  55.6 16.9 %collective-permute-done.1 = f32[4,512]{1,0:T(4,128)S(1)} collective-permute-done((f32[4,512]{1,0:T(4,128)S(1)}, f32[4,512]{1,0:T(4,128)S(1)}, u32[]{:S(2)}, u32[]{:S(2)}) %collective-permute-start.1) | collective-permute-done | bytes 8224 | tf_op jit(solution)/shard_map/while/body/eval_jaxpr/ppermute | solution.py:14
  72.6 1.3 fusion.86
  73.9 7.7 %fusion.87 = (f32[4,512]{1,0:T(4,128)S(1)}, f32[4,512,2112]{1,2,0:T(8,128)}) fusion(pred[512,2112]{0,1:T(8,128)(4,1)S(1)} %fusion.86, bf16[4,512,64]{1,2,0:T(8,128)(2,1)S(1)} %copy.57, bf16[4,2112,64]{1,2,0:T(8,128)(2,1)S(1)} %get-tuple-element.480), kind=kOutput, calls=%fused_computation.4.clone.1 | convolution fusion | flops 566622208 | bytes 19734528 | tf_op jit(solution)/shard_map/while/body/eval_jaxpr/hrd,hkd->hrk/dot_general | solution.py:67
  81.6 9.6 %fusion.88 = f32[4,512]{1,0:T(4,128)S(1)} fusion(f32[4,512,2112]{1,2,0:T(8,128)} %get-tuple-element.439, f32[4,512]{1,0:T(4,128)S(1)} %max.12, pred[512,2112]{0,1:T(8,128)(4,1)S(1)} %fusion.86), kind=kLoop, calls=%fused_computation.6.clone.1 | loop fusion | flops 17299456 | bytes 18399232 | tf_op jit(solution)/shard_map/while/body/eval_jaxpr/reduce_sum | solution.py:72
  91.2 11.6 %fusion.89 = f32[4,512,64]{1,2,0:T(8,128)} fusion(bf16[4,2112,64]{1,2,0:T(8,128)(2,1)} %get-tuple-element.481, f32[4,512,2112]{1,2,0:T(8,128)} %get-tuple-element.439, f32[4,512]{1,0:T(4,128)S(1)} %max.12, pred[512,2112]{0,1:T(8,128)(4,1)S(1)} %fusion.86, f32[4,512,64]{1,2,0:T(8,128)S(1)} %get-tuple-element.462, f32[4,512]{1,0:T(4,128)S(1)} %get-tuple-element.441), kind=kOutput, calls=%fused_computation.15.clone.1 | convolution fusion | flops 571211776 | bytes 20529152 | tf_op jit(solution)/shard_map/while/body/eval_jaxpr/hrk,hkd->hrd/dot_general | solution.py:73
  102.8 1.3 collective-permute-start
  104.1 1.6 collective-permute-start.1
  105.7 2.1 collective-permute-start.2
  107.8 16.0 %collective-permute-done.1 = f32[4,512]{1,0:T(4,128)S(1)} collective-permute-done((f32[4,512]{1,0:T(4,128)S(1)}, f32[4,512]{1,0:T(4,128)S(1)}, u32[]{:S(2)}, u32[]{:S(2)}) %collective-permute-start.1) | collective-permute-done | bytes 8224 | tf_op jit(solution)/shard_map/while/body/eval_jaxpr/ppermute | solution.py:14
  123.9 1.3 fusion.86
  125.2 7.7 %fusion.87 = (f32[4,512]{1,0:T(4,128)S(1)}, f32[4,512,2112]{1,2,0:T(8,128)}) fusion(pred[512,2112]{0,1:T(8,128)(4,1)S(1)} %fusion.86, bf16[4,512,64]{1,2,0:T(8,128)(2,1)S(1)} %copy.57, bf16[4,2112,64]{1,2,0:T(8,128)(2,1)S(1)} %get-tuple-element.480), kind=kOutput, calls=%fused_computation.4.clone.1 | convolution fusion | flops 566622208 | bytes 19734528 | tf_op jit(solution)/shard_map/while/body/eval_jaxpr/hrd,hkd->hrk/dot_general | solution.py:67
  133.0 9.6 %fusion.88 = f32[4,512]{1,0:T(4,128)S(1)} fusion(f32[4,512,2112]{1,2,0:T(8,128)} %get-tuple-element.439, f32[4,512]{1,0:T(4,128)S(1)} %max.12, pred[512,2112]{0,1:T(8,128)(4,1)S(1)} %fusion.86), kind=kLoop, calls=%fused_computation.6.clone.1 | loop fusion | flops 17299456 | bytes 18399232 | tf_op jit(solution)/shard_map/while/body/eval_jaxpr/reduce_sum | solution.py:72
  142.5 11.6 %fusion.89 = f32[4,512,64]{1,2,0:T(8,128)} fusion(bf16[4,2112,64]{1,2,0:T(8,128)(2,1)} %get-tuple-element.481, f32[4,512,2112]{1,2,0:T(8,128)} %get-tuple-element.439, f32[4,512]{1,0:T(4,128)S(1)} %max.12, pred[512,2112]{0,1:T(8,128)(4,1)S(1)} %fusion.86, f32[4,512,64]{1,2,0:T(8,128)S(1)} %get-tuple-element.462, f32[4,512]{1,0:T(4,128)S(1)} %get-tuple-element.441), kind=kOutput, calls=%fused_computation.15.clone.1 | convolution fusion | flops 571211776 | bytes 20529152 | tf_op jit(solution)/shard_map/while/body/eval_jaxpr/hrk,hkd->hrd/dot_general | solution.py:73
  154.1 0.8 collective-permute-start.1
  154.9 4.2 %collective-permute-start.2 = (f32[4,512]{1,0:T(4,128)S(1)}, f32[4,512]{1,0:T(4,128)S(1)}, u32[]{:S(2)}, u32[]{:S(2)}) collective-permute-start(f32[4,512]{1,0:T(4,128)S(1)} %get-tuple-element.440), channel_id=1, source_target_pairs={{6,0},{0,2},{2,4},{4,6},{7,1},{1,3},{3,5},{5,7},{14,8},{8,10},{10,... | collective-permute-start | bytes 24584 | tf_op jit(solution)/shard_map/while/body/eval_jaxpr/ppermute | solution.py:14
  159.1 15.2 %collective-permute-done.1 = f32[4,512]{1,0:T(4,128)S(1)} collective-permute-done((f32[4,512]{1,0:T(4,128)S(1)}, f32[4,512]{1,0:T(4,128)S(1)}, u32[]{:S(2)}, u32[]{:S(2)}) %collective-permute-start.1) | collective-permute-done | bytes 8224 | tf_op jit(solution)/shard_map/while/body/eval_jaxpr/ppermute | solution.py:14
  174.4 1.3 fusion.86
  175.7 7.7 %fusion.87 = (f32[4,512]{1,0:T(4,128)S(1)}, f32[4,512,2112]{1,2,0:T(8,128)}) fusion(pred[512,2112]{0,1:T(8,128)(4,1)S(1)} %fusion.86, bf16[4,512,64]{1,2,0:T(8,128)(2,1)S(1)} %copy.57, bf16[4,2112,64]{1,2,0:T(8,128)(2,1)S(1)} %get-tuple-element.480), kind=kOutput, calls=%fused_computation.4.clone.1 | convolution fusion | flops 566622208 | bytes 19734528 | tf_op jit(solution)/shard_map/while/body/eval_jaxpr/hrd,hkd->hrk/dot_general | solution.py:67
  183.4 9.6 %fusion.88 = f32[4,512]{1,0:T(4,128)S(1)} fusion(f32[4,512,2112]{1,2,0:T(8,128)} %get-tuple-element.439, f32[4,512]{1,0:T(4,128)S(1)} %max.12, pred[512,2112]{0,1:T(8,128)(4,1)S(1)} %fusion.86), kind=kLoop, calls=%fused_computation.6.clone.1 | loop fusion | flops 17299456 | bytes 18399232 | tf_op jit(solution)/shard_map/while/body/eval_jaxpr/reduce_sum | solution.py:72
  193.0 11.6 %fusion.89 = f32[4,512,64]{1,2,0:T(8,128)} fusion(bf16[4,2112,64]{1,2,0:T(8,128)(2,1)} %get-tuple-element.481, f32[4,512,2112]{1,2,0:T(8,128)} %get-tuple-element.439, f32[4,512]{1,0:T(4,128)S(1)} %max.12, pred[512,2112]{0,1:T(8,128)(4,1)S(1)} %fusion.86, f32[4,512,64]{1,2,0:T(8,128)S(1)} %get-tuple-element.462, f32[4,512]{1,0:T(4,128)S(1)} %get-tuple-element.441), kind=kOutput, calls=%fused_computation.15.clone.1 | convolution fusion | flops 571211776 | bytes 20529152 | tf_op jit(solution)/shard_map/while/body/eval_jaxpr/hrk,hkd->hrd/dot_general | solution.py:73
  204.6 0.7 collective-permute-start.1
  205.3 4.3 %collective-permute-start.2 = (f32[4,512]{1,0:T(4,128)S(1)}, f32[4,512]{1,0:T(4,128)S(1)}, u32[]{:S(2)}, u32[]{:S(2)}) collective-permute-start(f32[4,512]{1,0:T(4,128)S(1)} %get-tuple-element.440), channel_id=1, source_target_pairs={{6,0},{0,2},{2,4},{4,6},{7,1},{1,3},{3,5},{5,7},{14,8},{8,10},{10,... | collective-permute-start | bytes 24584 | tf_op jit(solution)/shard_map/while/body/eval_jaxpr/ppermute | solution.py:14
  209.5 14.3 %collective-permute-done.1 = f32[4,512]{1,0:T(4,128)S(1)} collective-permute-done((f32[4,512]{1,0:T(4,128)S(1)}, f32[4,512]{1,0:T(4,128)S(1)}, u32[]{:S(2)}, u32[]{:S(2)}) %collective-permute-start.1) | collective-permute-done | bytes 8224 | tf_op jit(solution)/shard_map/while/body/eval_jaxpr/ppermute | solution.py:14
  225.4 8.8 %convolution_convert_fusion.1 = bf16[64,2880]{1,0:T(8,128)(2,1)} fusion(bf16[64,2048]{1,0:T(8,128)(2,1)S(1)} %reshape.172, bf16[2048,2880]{0,1:T(8,128)(2,1)} %param.21), kind=kOutput, calls=%fused_computation.31 | convolution fusion | flops 755159040 | bytes 12427264 | tf_op jit(solution)/shard_map/dot_general | solution.py:91
  235.8 21.4 %all-reduce.2.cloned.1.call-done = bf16[64,2880]{1,0:T(8,128)(2,1)} async-done(((bf16[64,2880]{1,0:T(8,128)(2,1)}), bf16[64,2880]{1,0:T(8,128)(2,1)}) %all-reduce.2.cloned.1.call-update) | async-done | bytes 368656 | tf_op jit(solution)/shard_map/psum | solution.py:94
  257.3 2.1 convert_add_fusion
  259.4 1.7 convolution_convert_fusion
  261.1 1.0 copy.45
  262.1 42.1 %all_to_all.17 = bf16[16,16,2880]{2,1,0:T(8,128)(2,1)S(1)} all-to-all(bf16[16,16,2880]{2,1,0:T(8,128)(2,1)S(1)} %bitcast.102), channel_id=1, replica_groups=mesh['seq'=4,'ctx'=4,'head'=2] {'seq','ctx'}, dimensions={0} | all-to-all | bytes 2949120 | tf_op jit(solution)/shard_map/all_to_all | solution.py:113
  304.1 5.9 %fusion.25 = f32[256,1440]{0,1:T(8,128)S(1)} fusion(bf16[256,2880]{1,0:T(8,128)(2,1)S(1)} %bitcast.105, bf16[1,2880,1440]{1,2,0:T(8,128)(2,1)} %param.25), kind=kOutput, calls=%fused_computation.26 | convolution fusion | flops 2123366400 | bytes 11243520 | tf_op jit(solution)/shard_map/dot_general | solution.py:115
  310.0 16.2 %fusion.30 = bf16[2880,256]{1,0:T(8,128)(2,1)} fusion(bf16[1,1440,2880]{2,1,0:T(8,128)(2,1)} %param.27, bf16[256,2880]{1,0:T(8,128)(2,1)S(1)} %bitcast.106, bf16[1,2880,1440]{1,2,0:T(8,128)(2,1)} %param.26, f32[256,1440]{0,1:T(8,128)S(1)} %fusion.25), kind=kOutput, calls=%fused_computation.30 | convolution fusion | flops 4250419200 | bytes 21012480 | tf_op jit(solution)/shard_map/fd,rf->dr/dot_general | solution.py:120
  326.3 23.0 %reduce-scatter.2.cloned.1.call-done = bf16[1440,256]{1,0:T(8,128)(2,1)} async-done(((bf16[2880,256]{1,0:T(8,128)(2,1)}), bf16[1440,256]{1,0:T(8,128)(2,1)}) %reduce-scatter.2.cloned.1.call-update) | async-done | bytes 737296 | tf_op jit(solution)/shard_map/reduce_scatter | solution.py:119
  349.3 2.3 copy.46
  351.6 5.6 %all-to-all-start.1 = ((bf16[1440,16,16]{0,2,1:T(8,128)(2,1)}), bf16[1440,16,16]{0,2,1:T(8,128)(2,1)S(1)}, u32[]{:S(2)}, u32[]{:S(2)}) async-start(bf16[1440,16,16]{0,2,1:T(8,128)(2,1)} %bitcast.20), calls=%async_computation.2 | async-start | bytes 1572864 | tf_op jit(solution)/shard_map/all_to_all | solution.py:127
  357.4 21.1 %all-to-all-done.1 = bf16[1440,16,16]{0,2,1:T(8,128)(2,1)S(1)} async-done(((bf16[1440,16,16]{0,2,1:T(8,128)(2,1)}), bf16[1440,16,16]{0,2,1:T(8,128)(2,1)S(1)}, u32[]{:S(2)}, u32[]{:S(2)}) %all-to-all-start.1) | async-done | bytes 737312 | tf_op jit(solution)/shard_map/all_to_all | solution.py:127
  378.4 1.2 fusion.44
  (74 shorter events, 4.8 us)
Async XLA Ops:
  6.5 250.7 %all-reduce.2.cloned.1.call-start = ((), (), s32[]{:S(2)}) async-start(), calls=%async_computation.3 | async-start | bytes 753664 | tf_op jit(solution)/shard_map/psum | solution.py:94
  15.2 1.2 copy-start.2
  49.4 23.2 %collective-permute-start.3 = (f32[4,512,64]{1,2,0:T(8,128)}, f32[4,512,64]{1,2,0:T(8,128)S(1)}, u32[]{:S(2)}, u32[]{:S(2)}) collective-permute-start(f32[4,512,64]{1,2,0:T(8,128)} %fusion.89), channel_id=1, source_target_pairs={{6,0},{0,2},{2,4},{4,6},{7,1},{1,3},{3,5},{5,7},{14,8},{8,10},{10,... | collective-permute-start | bytes 1572872 | tf_op jit(solution)/shard_map/while/body/eval_jaxpr/ppermute | solution.py:14
  52.4 20.1 %collective-permute-start = (bf16[4,512,64]{1,2,0:T(8,128)(2,1)S(1)}, bf16[4,512,64]{1,2,0:T(8,128)(2,1)S(1)}, u32[]{:S(2)}, u32[]{:S(2)}) collective-permute-start(bf16[4,512,64]{1,2,0:T(8,128)(2,1)S(1)} %copy.57), channel_id=1, source_target_pairs={{6,0},{0,2},{2,4},{4,6},{7,1},{1,3},{3,5},{5,7},{14,8},{8,10},{10,... | collective-permute-start | bytes 786440 | tf_op jit(solution)/shard_map/while/body/eval_jaxpr/ppermute | solution.py:14
  54.0 18.5 %collective-permute-start.1 = (f32[4,512]{1,0:T(4,128)S(1)}, f32[4,512]{1,0:T(4,128)S(1)}, u32[]{:S(2)}, u32[]{:S(2)}) collective-permute-start(f32[4,512]{1,0:T(4,128)S(1)} %max.12), channel_id=1, source_target_pairs={{6,0},{0,2},{2,4},{4,6},{7,1},{1,3},{3,5},{5,7},{14,8},{8,10},{10,... | collective-permute-start | bytes 24584 | tf_op jit(solution)/shard_map/while/body/eval_jaxpr/ppermute | solution.py:14
  55.6 17.0 %collective-permute-start.2 = (f32[4,512]{1,0:T(4,128)S(1)}, f32[4,512]{1,0:T(4,128)S(1)}, u32[]{:S(2)}, u32[]{:S(2)}) collective-permute-start(f32[4,512]{1,0:T(4,128)S(1)} %get-tuple-element.440), channel_id=1, source_target_pairs={{6,0},{0,2},{2,4},{4,6},{7,1},{1,3},{3,5},{5,7},{14,8},{8,10},{10,... | collective-permute-start | bytes 24584 | tf_op jit(solution)/shard_map/while/body/eval_jaxpr/ppermute | solution.py:14
  102.8 21.1 %collective-permute-start.3 = (f32[4,512,64]{1,2,0:T(8,128)}, f32[4,512,64]{1,2,0:T(8,128)S(1)}, u32[]{:S(2)}, u32[]{:S(2)}) collective-permute-start(f32[4,512,64]{1,2,0:T(8,128)} %fusion.89), channel_id=1, source_target_pairs={{6,0},{0,2},{2,4},{4,6},{7,1},{1,3},{3,5},{5,7},{14,8},{8,10},{10,... | collective-permute-start | bytes 1572872 | tf_op jit(solution)/shard_map/while/body/eval_jaxpr/ppermute | solution.py:14
  102.8 21.1 %collective-permute-start = (bf16[4,512,64]{1,2,0:T(8,128)(2,1)S(1)}, bf16[4,512,64]{1,2,0:T(8,128)(2,1)S(1)}, u32[]{:S(2)}, u32[]{:S(2)}) collective-permute-start(bf16[4,512,64]{1,2,0:T(8,128)(2,1)S(1)} %copy.57), channel_id=1, source_target_pairs={{6,0},{0,2},{2,4},{4,6},{7,1},{1,3},{3,5},{5,7},{14,8},{8,10},{10,... | collective-permute-start | bytes 786440 | tf_op jit(solution)/shard_map/while/body/eval_jaxpr/ppermute | solution.py:14
  104.1 19.7 %collective-permute-start.1 = (f32[4,512]{1,0:T(4,128)S(1)}, f32[4,512]{1,0:T(4,128)S(1)}, u32[]{:S(2)}, u32[]{:S(2)}) collective-permute-start(f32[4,512]{1,0:T(4,128)S(1)} %max.12), channel_id=1, source_target_pairs={{6,0},{0,2},{2,4},{4,6},{7,1},{1,3},{3,5},{5,7},{14,8},{8,10},{10,... | collective-permute-start | bytes 24584 | tf_op jit(solution)/shard_map/while/body/eval_jaxpr/ppermute | solution.py:14
  105.7 18.2 %collective-permute-start.2 = (f32[4,512]{1,0:T(4,128)S(1)}, f32[4,512]{1,0:T(4,128)S(1)}, u32[]{:S(2)}, u32[]{:S(2)}) collective-permute-start(f32[4,512]{1,0:T(4,128)S(1)} %get-tuple-element.440), channel_id=1, source_target_pairs={{6,0},{0,2},{2,4},{4,6},{7,1},{1,3},{3,5},{5,7},{14,8},{8,10},{10,... | collective-permute-start | bytes 24584 | tf_op jit(solution)/shard_map/while/body/eval_jaxpr/ppermute | solution.py:14
  154.1 20.2 %collective-permute-start.3 = (f32[4,512,64]{1,2,0:T(8,128)}, f32[4,512,64]{1,2,0:T(8,128)S(1)}, u32[]{:S(2)}, u32[]{:S(2)}) collective-permute-start(f32[4,512,64]{1,2,0:T(8,128)} %fusion.89), channel_id=1, source_target_pairs={{6,0},{0,2},{2,4},{4,6},{7,1},{1,3},{3,5},{5,7},{14,8},{8,10},{10,... | collective-permute-start | bytes 1572872 | tf_op jit(solution)/shard_map/while/body/eval_jaxpr/ppermute | solution.py:14
  154.1 20.2 %collective-permute-start = (bf16[4,512,64]{1,2,0:T(8,128)(2,1)S(1)}, bf16[4,512,64]{1,2,0:T(8,128)(2,1)S(1)}, u32[]{:S(2)}, u32[]{:S(2)}) collective-permute-start(bf16[4,512,64]{1,2,0:T(8,128)(2,1)S(1)} %copy.57), channel_id=1, source_target_pairs={{6,0},{0,2},{2,4},{4,6},{7,1},{1,3},{3,5},{5,7},{14,8},{8,10},{10,... | collective-permute-start | bytes 786440 | tf_op jit(solution)/shard_map/while/body/eval_jaxpr/ppermute | solution.py:14
  154.1 20.1 %collective-permute-start.1 = (f32[4,512]{1,0:T(4,128)S(1)}, f32[4,512]{1,0:T(4,128)S(1)}, u32[]{:S(2)}, u32[]{:S(2)}) collective-permute-start(f32[4,512]{1,0:T(4,128)S(1)} %max.12), channel_id=1, source_target_pairs={{6,0},{0,2},{2,4},{4,6},{7,1},{1,3},{3,5},{5,7},{14,8},{8,10},{10,... | collective-permute-start | bytes 24584 | tf_op jit(solution)/shard_map/while/body/eval_jaxpr/ppermute | solution.py:14
  154.9 19.4 %collective-permute-start.2 = (f32[4,512]{1,0:T(4,128)S(1)}, f32[4,512]{1,0:T(4,128)S(1)}, u32[]{:S(2)}, u32[]{:S(2)}) collective-permute-start(f32[4,512]{1,0:T(4,128)S(1)} %get-tuple-element.440), channel_id=1, source_target_pairs={{6,0},{0,2},{2,4},{4,6},{7,1},{1,3},{3,5},{5,7},{14,8},{8,10},{10,... | collective-permute-start | bytes 24584 | tf_op jit(solution)/shard_map/while/body/eval_jaxpr/ppermute | solution.py:14
  204.6 19.4 %collective-permute-start.3 = (f32[4,512,64]{1,2,0:T(8,128)}, f32[4,512,64]{1,2,0:T(8,128)S(1)}, u32[]{:S(2)}, u32[]{:S(2)}) collective-permute-start(f32[4,512,64]{1,2,0:T(8,128)} %fusion.89), channel_id=1, source_target_pairs={{6,0},{0,2},{2,4},{4,6},{7,1},{1,3},{3,5},{5,7},{14,8},{8,10},{10,... | collective-permute-start | bytes 1572872 | tf_op jit(solution)/shard_map/while/body/eval_jaxpr/ppermute | solution.py:14
  204.6 19.4 %collective-permute-start = (bf16[4,512,64]{1,2,0:T(8,128)(2,1)S(1)}, bf16[4,512,64]{1,2,0:T(8,128)(2,1)S(1)}, u32[]{:S(2)}, u32[]{:S(2)}) collective-permute-start(bf16[4,512,64]{1,2,0:T(8,128)(2,1)S(1)} %copy.57), channel_id=1, source_target_pairs={{6,0},{0,2},{2,4},{4,6},{7,1},{1,3},{3,5},{5,7},{14,8},{8,10},{10,... | collective-permute-start | bytes 786440 | tf_op jit(solution)/shard_map/while/body/eval_jaxpr/ppermute | solution.py:14
  204.6 19.3 %collective-permute-start.1 = (f32[4,512]{1,0:T(4,128)S(1)}, f32[4,512]{1,0:T(4,128)S(1)}, u32[]{:S(2)}, u32[]{:S(2)}) collective-permute-start(f32[4,512]{1,0:T(4,128)S(1)} %max.12), channel_id=1, source_target_pairs={{6,0},{0,2},{2,4},{4,6},{7,1},{1,3},{3,5},{5,7},{14,8},{8,10},{10,... | collective-permute-start | bytes 24584 | tf_op jit(solution)/shard_map/while/body/eval_jaxpr/ppermute | solution.py:14
  205.3 18.7 %collective-permute-start.2 = (f32[4,512]{1,0:T(4,128)S(1)}, f32[4,512]{1,0:T(4,128)S(1)}, u32[]{:S(2)}, u32[]{:S(2)}) collective-permute-start(f32[4,512]{1,0:T(4,128)S(1)} %get-tuple-element.440), channel_id=1, source_target_pairs={{6,0},{0,2},{2,4},{4,6},{7,1},{1,3},{3,5},{5,7},{14,8},{8,10},{10,... | collective-permute-start | bytes 24584 | tf_op jit(solution)/shard_map/while/body/eval_jaxpr/ppermute | solution.py:14
  225.4 8.9 %copy-start.4 = (s32[1,64,4]{1,2,0:T(4,128)S(1)}, s32[1,64,4]{1,2,0:T(4,128)}, u32[]{:S(2)}) copy-start(s32[1,64,4]{1,2,0:T(4,128)} %param.23) | copy-start | bytes 3076
  225.4 31.9 %copy-start = (bf16[1,64,2880]{2,1,0:T(8,128)(2,1)S(1)}, bf16[1,64,2880]{2,1,0:T(8,128)(2,1)}, u32[]{:S(2)}) copy-start(bf16[1,64,2880]{2,1,0:T(8,128)(2,1)} %param.15) | copy-start | bytes 1105924
  234.2 25.2 %copy-start.3 = (f32[2880]{0:T(1024)S(1)}, f32[2880]{0:T(1024)}, u32[]{:S(2)}) copy-start(f32[2880]{0:T(1024)} %param.22) | copy-start | bytes 34564
  234.2 115.1 %reduce-scatter.2.cloned.1.call-start = ((), (), s32[]{:S(2)}) async-start(), calls=%async_computation.4 | async-start | bytes 2211840 | tf_op jit(solution)/shard_map/reduce_scatter | solution.py:119
  326.3 30.9 %copy-start.5 = (f32[1,64,4]{1,2,0:T(4,128)S(1)}, f32[1,64,4]{1,2,0:T(4,128)}, u32[]{:S(2)}) copy-start(f32[1,64,4]{1,2,0:T(4,128)} %param.24) | copy-start | bytes 3076
  326.3 52.2 %copy-start.1 = (f32[64,2880]{1,0:T(8,128)S(1)}, f32[64,2880]{1,0:T(8,128)}, u32[]{:S(2)}) copy-start(f32[64,2880]{1,0:T(8,128)} %get-tuple-element.355) | copy-start | bytes 2211844
  351.6 26.8 %all-to-all-start.1 = ((bf16[1440,16,16]{0,2,1:T(8,128)(2,1)}), bf16[1440,16,16]{0,2,1:T(8,128)(2,1)S(1)}, u32[]{:S(2)}, u32[]{:S(2)}) async-start(bf16[1440,16,16]{0,2,1:T(8,128)(2,1)} %bitcast.20), calls=%async_computation.2 | async-start | bytes 1572864 | tf_op jit(solution)/shard_map/all_to_all | solution.py:127
Sparse Core Ops, SparseCore 0:
  234.3 22.8 all-reduce.1
  326.4 22.8 reduce-scatter.1
where the time goes:
time: 387 us; the launch traced here: 386 us
  waiting for transfers between devices  128 us (33%)
  matrix products  118 us (30%)
  other arithmetic  49.5 us (13%)
  blocking collectives  42.1 us (11%)
  starting transfers between devices  26.7 us (7%)
  between operations  13.6 us (4%)
  local copies, waits for them, and re-layouts  8.03 us (2%)
    ppermute x16, waiting for transfers between devices, passed_along(): return lax.ppermute(block, axis, route)  62.7 us
    dot_general x4, matrix products, absorb(): jnp.einsum('hrk,hkd->hrd', weights.astype(jnp.bfloat16), values, preferre...  46.3 us
    all_to_all x1, blocking collectives, body(): lax.all_to_all(packed, ('seq', 'ctx'), split_axis=0, concat_axis=0, tiled...  42.1 us
    reduce_sum x4, other arithmetic, absorb(): total = total * fade + jnp.sum(weights, axis=-1)  38.2 us
    dot_general x4, matrix products, absorb(): jnp.einsum('hrd,hkd->hrk', block, keys, preferred_element_type=jnp.float32)  30.9 us
    reduce_scatter x1, waiting for transfers between devices, body(): lax.psum_scatter(jnp.einsum('fd,rf->dr', columns, hidden, preferred_eleme...  23 us
    psum x1, waiting for transfers between devices, body(): lax.psum(projected.astype(jnp.bfloat16), 'head').astype(jnp.float32)  21.4 us
    ppermute x16, starting transfers between devices, passed_along(): return lax.ppermute(block, axis, route)  21.1 us
  transfers between devices with their start and end apart: 19, of which 11 were waited for; matrix products, arithmetic and copies ran while one was open for 0% of the time, Pallas kernels for 0%

commit v1 on v0

v1 whole, which is shorter than its diff:
```python
import math, functools
import jax, jax.numpy as jnp
from jax import lax
from jax.experimental import pallas as pl
from jax.experimental.pallas import tpu as pltpu
from jax.sharding import PartitionSpec as P


CAP = 16
TILE = 256
LANES = 128
NEG = -1e38


def attend_kernel(where_ref, q_ref, kk_ref, vv_ref, nk_ref, nv_ref, out_ref, s_ref, m_ref, *, tokens, kv, pairs, tile):
    half = LANES // 2
    rows = tokens * pairs * 2
    length = kk_ref.shape[2]
    tiles = length // tile
    factor = math.log2(math.e) / math.sqrt(half)
    place, source = where_ref[0], where_ref[1]

    def queries(h):
        lane = lax.broadcasted_iota(jnp.int32, (tokens, LANES), 1)
        pieces = []
        for p in range(pairs):
            start = pl.multiple_of((h * pairs + p) * LANES, LANES)
            block = q_ref[:, pl.ds(start, LANES)]
            pieces.append(jnp.where(lane < half, block, jnp.zeros_like(block)))
            pieces.append(jnp.where(lane < half, jnp.zeros_like(block), block))
        return jnp.concatenate(pieces, axis=0)

    def score_tile(h, slot, q, j, top):
        keys = kk_ref[h, :, j * tile:(j + 1) * tile]
        s = jnp.dot(q, jnp.concatenate([keys, keys], axis=0), preferred_element_type=jnp.float32)
        s_ref[slot, :, j * tile:(j + 1) * tile] = s
        for k in range(tile // LANES):
            part = s[:, k * LANES:(k + 1) * LANES]
            top = part if top is None else jnp.maximum(top, part)
        return top

    def score_new(h, slot, q, top):
        keys = nk_ref[h]
        s = jnp.dot(q, jnp.concatenate([keys, keys], axis=0), preferred_element_type=jnp.float32)
        col = lax.broadcasted_iota(jnp.int32, (rows, LANES), 1)
        tok = lax.broadcasted_iota(jnp.int32, (rows, LANES), 0) % tokens
        reach = jnp.where(place < source, tokens, jnp.where(place == source, 0, -tokens))
        s = jnp.where((col < tokens) & (col <= tok + reach), s, NEG)
        s_ref[slot, :, length:] = s
        top = jnp.maximum(top, s)
        m_ref[slot] = jnp.broadcast_to(jnp.max(top, axis=1, keepdims=True) * factor, (rows, LANES))

    def weigh(slot, start, width):
        m = m_ref[slot]
        out = []
        for k in range(width // LANES):
            out.append(jnp.exp2(s_ref[slot, :, start + k * LANES:start + (k + 1) * LANES] * factor - m).astype(jnp.bfloat16))
        return out[0] if len(out) == 1 else jnp.concatenate(out, axis=1)

    def value_tile(h, slot, j, acc):
        p = weigh(slot, j * tile, tile)
        o = gather_values(p, vv_ref[h, :, j * tile:(j + 1) * tile])
        return o if acc is None else acc + o

    def gather_values(p, values):
        values = jnp.concatenate([values, jnp.ones_like(values)], axis=0)
        return lax.dot_general(p, values, (((1,), (1,)), ((), ())), preferred_element_type=jnp.float32)

    def finish(h, slot, acc):
        acc = acc + gather_values(weigh(slot, length, LANES), nv_ref[h])
        lane = lax.broadcasted_iota(jnp.int32, (tokens, LANES), 1)
        low = lane < half
        stats = out_ref[:, kv * pairs * LANES:]
        for p in range(pairs):
            even = acc[2 * p * tokens:(2 * p + 1) * tokens]
            odd = acc[(2 * p + 1) * tokens:(2 * p + 2) * tokens]
            num = jnp.where(low, even, pltpu.roll(odd, half, 1))
            tot = jnp.where(low, pltpu.roll(even, half, 1), odd)
            m = jnp.where(low, m_ref[slot, 2 * p * tokens:(2 * p + 1) * tokens], m_ref[slot, (2 * p + 1) * tokens:(2 * p + 2) * tokens])
            index = h * pairs + p
            out_ref[:, pl.ds(pl.multiple_of(index * LANES, LANES), LANES)] = (num / tot).astype(jnp.bfloat16)
            lse = m + jnp.log2(tot)
            for piece in range(3):
                coarse = lse.astype(jnp.bfloat16)
                lse = lse - coarse.astype(jnp.float32)
                stats = jnp.where(lane % half == index + piece * kv * pairs, coarse, stats)
        out_ref[:, kv * pairs * LANES:] = stats

    out_ref[:, kv * pairs * LANES:] = jnp.zeros((tokens, LANES), jnp.bfloat16)
    q = queries(0)
    top = None
    for j in range(tiles):
        top = score_tile(0, 0, q, j, top)
    score_new(0, 0, q, top)

    def step(h, carry):
        slot = h % 2
        prev = 1 - slot
        q = queries(h)
        top = acc = None
        for j in range(tiles):
            top = score_tile(h, slot, q, j, top)
            acc = value_tile(h - 1, prev, j, acc)
        score_new(h, slot, q, top)
        finish(h - 1, prev, acc)
        return carry

    lax.fori_loop(1, kv, step, 0)
    acc = None
    last = (kv - 1) % 2
    for j in range(tiles):
        acc = value_tile(kv - 1, last, j, acc)
    finish(kv - 1, last, acc)


def attend(place, source, q, kk, vv, nk, nv, tile=TILE):
    tokens, width = q.shape
    kv, _, length = kk.shape
    pairs = width // LANES // kv
    rows = tokens * pairs * 2
    where = jnp.stack([place, source]).astype(jnp.int32)
    vm = pl.BlockSpec(memory_space=pltpu.VMEM)
    flops = 4 * rows * kv * (length + LANES) * LANES
    return pl.pallas_call(
        functools.partial(attend_kernel, tokens=tokens, kv=kv, pairs=pairs, tile=tile),
        out_shape=jax.ShapeDtypeStruct((tokens, width + LANES), jnp.bfloat16),
        in_specs=[pl.BlockSpec(memory_space=pltpu.SMEM)] + [vm] * 5,
        out_specs=vm,
        scratch_shapes=[pltpu.VMEM((2, rows, length + LANES), jnp.float32), pltpu.VMEM((2, rows, LANES), jnp.float32)],
        compiler_params=pltpu.CompilerParams(vmem_limit_bytes=32 * 1024 * 1024),
        cost_estimate=pl.CostEstimate(flops=flops * 2, bytes_accessed=0, transcendentals=0),
        name="attend",
    )(where, q, kk, vv, nk, nv)


def merge_kernel(*refs, count, group):
    packets, weight_ref, out_ref, attn_ref = refs[:count], refs[count], refs[count + 1], refs[count + 2]
    tokens = packets[0].shape[0]
    width = packets[0].shape[1] - LANES

    @pl.when(pl.program_id(0) == 0)
    def _():
        logs = []
        for packet in packets:
            pieces = packet[:, width:].astype(jnp.float32)
            logs.append(pieces + (pltpu.roll(pieces, LANES - group, 1) + pltpu.roll(pieces, LANES - 2 * group, 1)))
        top = functools.reduce(jnp.maximum, logs)
        shares = [jnp.exp2(log - top) for log in logs]
        total = functools.reduce(jnp.add, shares)
        split = []
        for share in shares:
            share = share / total
            coarse = share.astype(jnp.bfloat16)
            split.append(jnp.concatenate([coarse, (share - coarse.astype(jnp.float32)).astype(jnp.bfloat16)], axis=1))
        split = jnp.concatenate(split, axis=0)
        half = LANES // 2
        lanes = 2 * LANES
        row = lax.broadcasted_iota(jnp.int32, (lanes, lanes), 0) % LANES
        col = lax.broadcasted_iota(jnp.int32, (lanes, lanes), 1)
        for start in range(0, width, lanes):
            head = (col + start) // LANES + col % LANES // half * half
            spread = jnp.where(row == head, 1.0, 0.0).astype(jnp.bfloat16)
            wide = jnp.dot(split, spread, preferred_element_type=jnp.float32)
            attn = 0.0
            for i, packet in enumerate(packets):
                attn = attn + wide[i * tokens:(i + 1) * tokens] * packet[:, start:start + lanes].astype(jnp.float32)
            attn_ref[:, start:start + lanes] = attn.astype(jnp.bfloat16)

    part = lax.dot_general(weight_ref[...], attn_ref[...], TURNED, preferred_element_type=jnp.float32)
    out_ref[...] = part.T.astype(out_ref.dtype)


def merge_project(packets, weight, group, block=5 * LANES):
    tokens = packets[0].shape[0]
    model, depth = weight.shape
    vm = pl.BlockSpec(memory_space=pltpu.VMEM)
    return pl.pallas_call(
        functools.partial(merge_kernel, count=len(packets), group=group),
        out_shape=jax.ShapeDtypeStruct((tokens, model), jnp.bfloat16),
        grid=(pl.cdiv(model, block),),
        in_specs=[vm] * len(packets) + [pl.BlockSpec((block, depth), lambda k: (k, 0))],
        out_specs=pl.BlockSpec((tokens, block), lambda k: (0, k)),
        scratch_shapes=[pltpu.VMEM((tokens, depth), jnp.bfloat16)],
        compiler_params=pltpu.CompilerParams(vmem_limit_bytes=58 * 1024 * 1024),
        cost_estimate=pl.CostEstimate(flops=2 * tokens * depth * model, bytes_accessed=2 * depth * model, transcendentals=0),
        name="merge_project",
    )(*packets, weight)


def steps_of(extent, step):
    return [(start, min(start + step, extent)) for start in range(0, extent, step)]


TURNED = (((1,), (1,)), ((), ()))


def expert_kernel(rows_ref, gate_hbm, up_hbm, down_hbm, out_ref, gate_ref, up_ref, down_ref, act_ref, acc_ref, sems, *, step):
    hidden, model = gate_hbm.shape
    pairs = []
    for start, stop in steps_of(hidden, step):
        pairs.append((gate_hbm.at[start:stop], gate_ref.at[start:stop]))
        pairs.append((up_hbm.at[start:stop], up_ref.at[start:stop]))
    later = len(pairs)
    for start, stop in steps_of(hidden, step):
        pairs.append((down_hbm.at[start:stop], down_ref.at[start:stop]))
    copies = [pltpu.make_async_copy(source, target, sems.at[i]) for i, (source, target) in enumerate(pairs)]
    for copy in copies:
        copy.start()
    rows = rows_ref[...]
    for i, (start, stop) in enumerate(steps_of(hidden, step)):
        copies[2 * i].wait()
        copies[2 * i + 1].wait()
        gate = lax.dot_general(gate_ref[start:stop], rows, TURNED, preferred_element_type=jnp.float32)
        up = lax.dot_general(up_ref[start:stop], rows, TURNED, preferred_element_type=jnp.float32)
        act = gate * jax.nn.sigmoid(1.702 * gate) * (up + 1.0)
        act_ref[:, start:stop] = act.T.astype(jnp.bfloat16)
    for copy in copies[later:]:
        copy.wait()
    act = act_ref[...]
    for start, stop in steps_of(model, 4 * LANES):
        acc_ref[:, start:stop] = jnp.dot(act, down_ref[:, start:stop], preferred_element_type=jnp.float32)
    width = out_ref.shape[2]
    for i in range(out_ref.shape[0]):
        out_ref[i] = acc_ref[:, i * width:(i + 1) * width].astype(out_ref.dtype)


def expert(rows, gate, up, down, pieces, step=2 * LANES):
    count, model = rows.shape
    hidden = gate.shape[0]
    vm = pl.BlockSpec(memory_space=pltpu.VMEM)
    stay = pl.BlockSpec(memory_space=pl.ANY)
    return pl.pallas_call(
        functools.partial(expert_kernel, step=step),
        out_shape=jax.ShapeDtypeStruct((pieces, count, model // pieces), jnp.bfloat16),
        in_specs=[vm] + [stay] * 3,
        out_specs=vm,
        scratch_shapes=[
            pltpu.VMEM((hidden, model), jnp.bfloat16),
            pltpu.VMEM((hidden, model), jnp.bfloat16),
            pltpu.VMEM((hidden, model), jnp.bfloat16),
            pltpu.VMEM((count, hidden), jnp.bfloat16),
            pltpu.VMEM((count, model), jnp.float32),
            pltpu.SemaphoreType.DMA((3 * pl.cdiv(hidden, step),)),
        ],
        compiler_params=pltpu.CompilerParams(vmem_limit_bytes=56 * 1024 * 1024),
        cost_estimate=pl.CostEstimate(flops=6 * count * model * hidden, bytes_accessed=6 * model * hidden, transcendentals=0),
        name="expert",
    )(rows, gate, up, down)


def project_kernel(x_ref, weight_ref, out_ref):
    out_ref[...] = jnp.dot(x_ref[...], weight_ref[...], preferred_element_type=jnp.float32).astype(out_ref.dtype)


def project(x, weight, block=2 * LANES):
    tokens, model = x.shape
    width = weight.shape[1]
    return pl.pallas_call(
        project_kernel,
        out_shape=jax.ShapeDtypeStruct((tokens, width), jnp.bfloat16),
        grid=(pl.cdiv(width, block),),
        in_specs=[pl.BlockSpec((tokens, model), lambda n: (0, 0)), pl.BlockSpec((model, block), lambda n: (0, n))],
        out_specs=pl.BlockSpec((tokens, block), lambda n: (0, n)),
        compiler_params=pltpu.CompilerParams(vmem_limit_bytes=58 * 1024 * 1024),
        cost_estimate=pl.CostEstimate(flops=2 * tokens * model * width, bytes_accessed=2 * model * width, transcendentals=0),
        name="project",
    )(x, weight)


def shifted(block, axis, distance):
    size = lax.axis_size(axis)
    return lax.ppermute(block, axis, [(i, (i + distance) % size) for i in range(size)])


def body(
    stream,
    query_weight,
    cache_keys,
    cache_values,
    new_keys,
    new_values,
    out_weight,
    norm_gain,
    expert_ids,
    expert_weights,
    gate_weight,
    up_weight,
    down_weight,
):
    tokens = stream[0]
    count, model = tokens.shape
    cycles = lax.axis_size("ctx")
    heads = lax.axis_size("head")
    place = lax.axis_index("ctx")
    query = project(tokens, query_weight)

    def columns(x):
        return x[0].transpose(1, 2, 0)

    def padded(x):
        return jnp.pad(x, ((0, 0), (0, 0), (0, LANES - x.shape[2])))

    keys, values = columns(cache_keys), columns(cache_values)
    fresh_keys, fresh_values = padded(columns(new_keys)), padded(columns(new_values))
    packets = []
    block = query
    for d in range(cycles):
        following = shifted(block, "ctx", 1) if d < cycles - 1 else None
        packet = attend(place, (place - d) % cycles, block, keys, values, fresh_keys, fresh_values)
        if d < cycles - 1:
            following, packet = lax.optimization_barrier((following, packet))
        packets.append(packet if d == 0 else shifted(packet, "ctx", -d))
        block = following
    group = query.shape[1] // LANES
    projected = merge_project(packets, out_weight.T, group)
    resid = tokens.astype(jnp.float32) + projected.astype(jnp.float32)
    for d in range(1, heads):
        resid = resid + shifted(projected, "head", d).astype(jnp.float32)
    width = model // heads
    resid_own = lax.dynamic_slice_in_dim(resid, lax.axis_index("head") * width, width, 1)
    normed = (
        resid * lax.rsqrt(jnp.mean(resid * resid, axis=-1, keepdims=True) + 1e-05) * norm_gain
    ).astype(jnp.bfloat16)
    experts = lax.axis_size("seq") * lax.axis_size("ctx")
    slots = experts * CAP
    chosen = expert_ids[0].reshape(-1)
    onehot = (chosen[:, None] == lax.broadcasted_iota(jnp.int32, (1, experts), 1)).astype(jnp.int32)
    before = jnp.cumsum(onehot, axis=0) - onehot
    target = chosen * CAP + jnp.sum(before * onehot, axis=1)
    matches = target[None, :] == lax.broadcasted_iota(jnp.int32, (slots, 1), 0)
    select = jnp.sum(matches.astype(jnp.float32).reshape(slots, count, -1), axis=-1).astype(jnp.bfloat16)
    packed = jnp.dot(select, normed, preferred_element_type=jnp.float32).astype(jnp.bfloat16)
    packed = packed.reshape(experts, CAP, model)
    arrived = lax.all_to_all(packed, ("seq", "ctx"), split_axis=0, concat_axis=0, tiled=True)
    parts = expert(arrived.reshape(slots, model), gate_weight[0].T, up_weight[0].T, down_weight[0], heads)
    parts = parts.reshape(heads * experts, CAP, width)
    returned = lax.all_to_all(parts, ("head", "seq", "ctx"), split_axis=0, concat_axis=0, tiled=True)
    spread = jnp.where(matches.T, expert_weights[0].reshape(-1)[:, None], 0.0)
    spread = jnp.sum(spread.reshape(count, -1, slots), axis=1)
    moe = lax.dot_general(
        jnp.tile(spread, (1, heads)),
        returned.reshape(heads * slots, width).astype(jnp.float32),
        (((1,), (0,)), ((), ())),
        precision=lax.Precision.HIGHEST,
    )
    return (resid_own + moe).astype(jnp.bfloat16)[None]


def solution(mesh):
    in_specs = (
        P("seq", "ctx", None),
        P(None, "head"),
        P("seq", "ctx", "head", None),
        P("seq", "ctx", "head", None),
        P("seq", "ctx", "head", None),
        P("seq", "ctx", "head", None),
        P("head", None),
        P(),
        P("seq", "ctx", None),
        P("seq", "ctx", None),
        P(("seq", "ctx"), None, "head"),
        P(("seq", "ctx"), None, "head"),
        P(("seq", "ctx"), "head", None),
    )
    out_specs = P("seq", "ctx", "head")
    return jax.shard_map(body, mesh=mesh, in_specs=in_specs, out_specs=out_specs, check_vma=False)
```

time: 387 us -> 200 us (0.52)
  matrix products: 118 us -> 3.41 us
  Pallas kernels: 0 us -> 70.1 us
  waiting for transfers between devices: 128 us -> 62.1 us
  other arithmetic: 49.5 us -> 2.53 us
  between operations: 13.6 us -> 0.26 us
  starting transfers between devices: 26.7 us -> 14.4 us
    dot_general x13 -> x1, matrix products: 116 us -> 1.59 us  [body(): lax.dot_general(jnp.tile(spread, (1, heads)), returned.reshape(heads * sl...]
    pallas_call x0 -> x7, Pallas kernels: none -> 70.1 us  [the longest x4 38.2 us: attend(): pl.pallas_call(functools.partial(attend_kernel, tokens=tokens, kv=kv, pai...]
    reduce_sum x5 -> x2, other arithmetic: 38.4 us -> 1.4 us  [the longest x1 1.26 us: body(): jnp.mean(resid * resid, axis=-1, keepdims=True) + 1e-05]
    ppermute x16 -> x7, waiting for transfers between devices: 62.7 us -> 26.5 us  [shifted(): lax.ppermute(block, axis, [(i, (i + distance) % size) for i in range(size)])]
    reduce_scatter x1 -> x0, waiting for transfers between devices: 23 us -> none  [body(): lax.psum_scatter(jnp.einsum('fd,rf->dr', columns, hidden, preferred_eleme...]
    psum x1 -> x0, waiting for transfers between devices: 21.4 us -> none  [body(): lax.psum(projected.astype(jnp.bfloat16), 'head').astype(jnp.float32)]
    all_to_all x1, waiting for transfers between devices: 21.1 us -> 35.6 us  [body(): lax.all_to_all(parts, ('head', 'seq', 'ctx'), split_axis=0, concat_axis=0...]
    ppermute x16 -> x7, starting transfers between devices: 21.1 us -> 11.1 us  [shifted(): lax.ppermute(block, axis, [(i, (i + distance) % size) for i in range(size)])]
  transfers between devices with their start and end apart: 19 -> 8, of which waited for: 11 -> 4; matrix products, arithmetic and copies ran while one was open for 0% -> 1% of each run, Pallas kernels for 0% -> 19%
where the time goes in v1:
time: 200 us; the launch traced here: 198 us
  Pallas kernels  70.1 us (35%)
  waiting for transfers between devices  62.1 us (31%)
  blocking collectives  40 us (20%)
  starting transfers between devices  14.4 us (7%)
  local copies, waits for them, and re-layouts  5.2 us (3%)
  matrix products  3.41 us (2%)
  other arithmetic  2.53 us (1%)
    all_to_all x1, blocking collectives, body(): lax.all_to_all(packed, ('seq', 'ctx'), split_axis=0, concat_axis=0, tiled...  40 us
    pallas_call x4, Pallas kernels, attend(): pl.pallas_call(functools.partial(attend_kernel, tokens=tokens, kv=kv, pai...  38.2 us
    all_to_all x1, waiting for transfers between devices, body(): lax.all_to_all(parts, ('head', 'seq', 'ctx'), split_axis=0, concat_axis=0...  35.6 us
    ppermute x7, waiting for transfers between devices, shifted(): lax.ppermute(block, axis, [(i, (i + distance) % size) for i in range(size)])  26.5 us
    pallas_call x1, Pallas kernels, expert(): pl.pallas_call(functools.partial(expert_kernel, step=step), out_shape=jax...  13.9 us
    ppermute x7, starting transfers between devices, shifted(): lax.ppermute(block, axis, [(i, (i + distance) % size) for i in range(size)])  11.1 us
    pallas_call x1, Pallas kernels, merge_project(): pl.pallas_call(functools.partial(merge_kernel, count=len(packets), group=...  9.07 us
    pallas_call x1, Pallas kernels, project(): pl.pallas_call(project_kernel, out_shape=jax.ShapeDtypeStruct((tokens, wi...  8.9 us
  transfers between devices with their start and end apart: 8, of which 4 were waited for; matrix products, arithmetic and copies ran while one was open for 1% of the time, Pallas kernels for 19%

profile of v1, /device:TPU:0, one launch (start us, length us, event | category | flops | bytes accessed | tf_op | source)
XLA Modules:
  0.0 198.0 jit_solution(4233160069079127551)
XLA Ops:
  0.0 8.9 %project.1.q_ref = bf16[64,2048]{1,0:T(8,128)(2,1)} custom-call(bf16[64,2880]{1,0:T(8,128)(2,1)} %bitcast.77, bf16[2880,2048]{1,0:T(8,128)(2,1)} %weight_ref.1), custom_call_target="tpu_custom_call" | custom-call | flops 754974720 | bytes 11796480 | tf_op jit(solution)/shard_map/project/pallas_call | solution.py:258
  8.9 3.1 %collective-permute-start = (bf16[64,2048]{1,0:T(8,128)(2,1)}, bf16[64,2048]{1,0:T(8,128)(2,1)S(1)}, u32[]{:S(2)}, u32[]{:S(2)}) collective-permute-start(bf16[64,2048]{1,0:T(8,128)(2,1)} %project.1.q_ref), channel_id=1, source_target_pairs={{0,2},{2,4},{4,6},{6,0},{1,3},{3,5},{5,7},{7,1},{8,10},{10,12},{12... | collective-permute-start | bytes 786440 | tf_op jit(solution)/shard_map/ppermute | solution.py:272
  12.0 0.1 copy.28
  12.1 0.1 copy.29
  12.3 0.1 pad_add_fusion.where_ref
  12.4 0.9 copy-done.1
  13.3 9.5 %attend.4.refs_0_ = bf16[64,2176]{1,0:T(8,128)(2,1)S(1)} custom-call(s32[2]{0:T(128)S(1)} %pad_add_fusion.where_ref, bf16[64,2048]{1,0:T(8,128)(2,1)S(1)} %copy-done.1, bf16[4,64,2048]{2,1,0:T(8,128)(2,1)S(1)} %bitcast.61, bf16[4,64,2048]{2,1,0:T(8,128)(2,1)S(1)} %bitcast.65, bf16[4,64,128]{2,1,0:T(8,128)(2,1)S(1)} %pad.7.nk_ref, ...), custom_call_target="tpu_custom_call" | custom-call | flops 4563402752 | tf_op jit(solution)/shard_map/attend/pallas_call | solution.py:124
  22.9 0.7 copy-done
  23.6 0.1 pad_add_fusion.1.where_ref
  23.7 0.1 copy.30
  23.8 0.1 eq.56
  23.9 0.1 eq.52
  24.0 0.1 pad_add_fusion.2.where_ref
  24.1 0.1 pad_add_fusion.3.where_ref
  24.1 0.0 collective-permute-done.q_ref
  24.1 1.6 collective-permute-start.1
  25.7 9.5 %attend.5 = bf16[64,2176]{1,0:T(8,128)(2,1)S(1)} custom-call(s32[2]{0:T(128)S(1)} %pad_add_fusion.1.where_ref, bf16[64,2048]{1,0:T(8,128)(2,1)S(1)} %collective-permute-done.q_ref, bf16[4,64,2048]{2,1,0:T(8,128)(2,1)S(1)} %bitcast.62, bf16[4,64,2048]{2,1,0:T(8,128)(2,1)S(1)} %bitcast.66, bf16[4,64,128]{2,1,0:T(8,128)(2,1)S(1)} %pad.7.nk_ref, ...), custom_call_target="tpu_custom_call" | custom-call | flops 4563402752 | tf_op jit(solution)/shard_map/attend/pallas_call | solution.py:124
  35.3 0.0 collective-permute-done.1.q_ref
  35.3 1.6 collective-permute-start.3
  36.9 2.2 %collective-permute-start.2 = (bf16[64,2176]{1,0:T(8,128)(2,1)S(1)}, bf16[64,2176]{1,0:T(8,128)(2,1)}, u32[]{:S(2)}, u32[]{:S(2)}) collective-permute-start(bf16[64,2176]{1,0:T(8,128)(2,1)S(1)} %attend.5), channel_id=1, source_target_pairs={{0,6},{2,0},{4,2},{6,4},{1,7},{3,1},{5,3},{7,5},{8,14},{10,8},{12,... | collective-permute-start | bytes 835592 | tf_op jit(solution)/shard_map/ppermute | solution.py:272
  39.2 9.5 %attend.6 = bf16[64,2176]{1,0:T(8,128)(2,1)S(1)} custom-call(s32[2]{0:T(128)S(1)} %pad_add_fusion.2.where_ref, bf16[64,2048]{1,0:T(8,128)(2,1)S(1)} %collective-permute-done.1.q_ref, bf16[4,64,2048]{2,1,0:T(8,128)(2,1)S(1)} %bitcast.63, bf16[4,64,2048]{2,1,0:T(8,128)(2,1)S(1)} %bitcast.67, bf16[4,64,128]{2,1,0:T(8,128)(2,1)S(1)} %pad.7.nk_ref, ...), custom_call_target="tpu_custom_call" | custom-call | flops 4563402752 | tf_op jit(solution)/shard_map/attend/pallas_call | solution.py:124
  48.7 0.0 collective-permute-done.3.q_ref
  48.7 9.5 %attend.7 = bf16[64,2176]{1,0:T(8,128)(2,1)S(1)} custom-call(s32[2]{0:T(128)S(1)} %pad_add_fusion.3.where_ref, bf16[64,2048]{1,0:T(8,128)(2,1)S(1)} %collective-permute-done.3.q_ref, bf16[4,64,2048]{2,1,0:T(8,128)(2,1)S(1)} %bitcast.64, bf16[4,64,2048]{2,1,0:T(8,128)(2,1)S(1)} %bitcast.68, bf16[4,64,128]{2,1,0:T(8,128)(2,1)S(1)} %pad.7.nk_ref, ...), custom_call_target="tpu_custom_call" | custom-call | flops 4563402752 | tf_op jit(solution)/shard_map/attend/pallas_call | solution.py:124
  58.3 0.1 collective-permute-start.5
  58.3 1.0 collective-permute-start.4
  59.3 0.6 reduce-window.6
  59.9 0.2 slice_reduce_fusion
  60.1 0.0 collective-permute-done.2.refs_1_
  60.1 9.6 %collective-permute-done.5.refs_3_ = bf16[64,2176]{1,0:T(8,128)(2,1)S(1)} collective-permute-done((bf16[64,2176]{1,0:T(8,128)(2,1)S(1)}, bf16[64,2176]{1,0:T(8,128)(2,1)S(1)}, u32[]{:S(2)}, u32[]{:S(2)}) %collective-permute-start.5) | collective-permute-done | bytes 278560 | tf_op jit(solution)/shard_map/ppermute | solution.py:272
  69.7 8.8 %collective-permute-done.4.refs_2_ = bf16[64,2176]{1,0:T(8,128)(2,1)S(1)} collective-permute-done((bf16[64,2176]{1,0:T(8,128)(2,1)S(1)}, bf16[64,2176]{1,0:T(8,128)(2,1)S(1)}, u32[]{:S(2)}, u32[]{:S(2)}) %collective-permute-start.4) | collective-permute-done | bytes 278560 | tf_op jit(solution)/shard_map/ppermute | solution.py:272
  78.5 0.7 copy-done.6
  79.2 9.1 %merge_project.1 = bf16[64,2880]{1,0:T(8,128)(2,1)} custom-call(bf16[64,2176]{1,0:T(8,128)(2,1)} %copy-done, bf16[64,2176]{1,0:T(8,128)(2,1)} %collective-permute-done.2.refs_1_, bf16[64,2176]{1,0:T(8,128)(2,1)} %copy-done.6, bf16[64,2176]{1,0:T(8,128)(2,1)} %copy-done.5, bf16[2880,2048]{1,0:T(8,128)(2,1)} %bitcast.69), custom_call_target="tpu_custom_call" | custom-call | flops 754974720 | bytes 11796480 | tf_op jit(solution)/shard_map/merge_project/pallas_call | solution.py:177
  88.3 1.5 collective-permute-start.6
  89.8 0.1 fusion.6
  89.9 0.1 reduce_sum.39
  90.0 0.1 copy.34
  90.1 0.1 convert_reduce_fusion
  90.2 8.2 %collective-permute-done.6 = bf16[64,2880]{1,0:T(8,128)(2,1)S(1)} collective-permute-done((bf16[64,2880]{1,0:T(8,128)(2,1)}, bf16[64,2880]{1,0:T(8,128)(2,1)S(1)}, u32[]{:S(2)}, u32[]{:S(2)}) %collective-permute-start.6) | collective-permute-done | bytes 368672 | tf_op jit(solution)/shard_map/ppermute | solution.py:272
  98.4 1.3 multiply_reduce_fusion
  99.7 1.8 convolution_convert_fusion
  101.5 1.8 copy.36
  103.3 40.0 %all_to_all.10 = bf16[16,16,2880]{2,1,0:T(8,128)(2,1)} all-to-all(bf16[16,16,2880]{2,1,0:T(8,128)(2,1)S(1)} %bitcast.75), channel_id=1, replica_groups=mesh['seq'=4,'ctx'=4,'head'=2] {'seq','ctx'}, dimensions={0} | all-to-all | bytes 2949120 | tf_op jit(solution)/shard_map/all_to_all | solution.py:334
  143.3 13.9 %expert.1 = bf16[2,256,1440]{2,1,0:T(8,128)(2,1)} custom-call(bf16[256,2880]{1,0:T(8,128)(2,1)} %bitcast.76, bf16[1440,2880]{1,0:T(8,128)(2,1)} %bitcast.70, bf16[1440,2880]{1,0:T(8,128)(2,1)} %bitcast.71, bf16[1440,2880]{1,0:T(8,128)(2,1)} %bitcast.72), custom_call_target="tpu_custom_call" | custom-call | flops 6370099200 | bytes 24883200 | tf_op jit(solution)/shard_map/expert/pallas_call | solution.py:232
  157.3 0.0 copy-start.11
  157.3 3.3 %all-to-all-start.1 = ((bf16[32,16,1440]{2,1,0:T(8,128)(2,1)}), bf16[32,16,1440]{2,1,0:T(8,128)(2,1)S(1)}, u32[]{:S(2)}, u32[]{:S(2)}) async-start(bf16[32,16,1440]{2,1,0:T(8,128)(2,1)} %bitcast.74), calls=%async_computation.1 | async-start | bytes 3145728 | tf_op jit(solution)/shard_map/all_to_all | solution.py:337
  160.6 0.1 select_reduce_fusion
  160.8 35.6 %all-to-all-done.1 = bf16[32,16,1440]{2,1,0:T(8,128)(2,1)S(1)} async-done(((bf16[32,16,1440]{2,1,0:T(8,128)(2,1)}), bf16[32,16,1440]{2,1,0:T(8,128)(2,1)S(1)}, u32[]{:S(2)}, u32[]{:S(2)}) %all-to-all-start.1) | async-done | bytes 1474592 | tf_op jit(solution)/shard_map/all_to_all | solution.py:337
  196.4 1.6 fusion.2
  (29 shorter events, 0.2 us)
Async XLA Ops:
  0.0 12.0 %copy-start.7 = (bf16[1,64,4,64]{3,2,1,0:T(4,128)(2,1)S(1)}, bf16[1,64,4,64]{3,2,1,0:T(4,128)(2,1)}, u32[]{:S(2)}) copy-start(bf16[1,64,4,64]{3,2,1,0:T(4,128)(2,1)} %param.17) | copy-start | bytes 98308
  0.0 12.1 %copy-start.8 = (bf16[1,64,4,64]{3,2,1,0:T(4,128)(2,1)S(1)}, bf16[1,64,4,64]{3,2,1,0:T(4,128)(2,1)}, u32[]{:S(2)}) copy-start(bf16[1,64,4,64]{3,2,1,0:T(4,128)(2,1)} %param.18) | copy-start | bytes 98308
  0.0 12.4 %copy-start.2 = (bf16[1,2048,4,64]{1,3,2,0:T(8,128)(2,1)S(1)}, bf16[1,2048,4,64]{1,3,2,0:T(8,128)(2,1)}, u32[]{:S(2)}) copy-start(bf16[1,2048,4,64]{1,3,2,0:T(8,128)(2,1)} %param.15) | copy-start | bytes 3145732
  0.0 12.4 %copy-start.3 = (bf16[1,2048,4,64]{1,3,2,0:T(8,128)(2,1)S(1)}, bf16[1,2048,4,64]{1,3,2,0:T(8,128)(2,1)}, u32[]{:S(2)}) copy-start(bf16[1,2048,4,64]{1,3,2,0:T(8,128)(2,1)} %param.16) | copy-start | bytes 3145732
  8.9 15.2 %collective-permute-start = (bf16[64,2048]{1,0:T(8,128)(2,1)}, bf16[64,2048]{1,0:T(8,128)(2,1)S(1)}, u32[]{:S(2)}, u32[]{:S(2)}) collective-permute-start(bf16[64,2048]{1,0:T(8,128)(2,1)} %project.1.q_ref), channel_id=1, source_target_pairs={{0,2},{2,4},{4,6},{6,0},{1,3},{3,5},{5,7},{7,1},{8,10},{10,12},{12... | collective-permute-start | bytes 786440 | tf_op jit(solution)/shard_map/ppermute | solution.py:272
  12.4 1.0 copy-start.1
  13.3 10.3 %copy-start.10 = (s32[1,64,4]{1,2,0:T(4,128)S(1)}, s32[1,64,4]{1,2,0:T(4,128)}, u32[]{:S(2)}) copy-start(s32[1,64,4]{1,2,0:T(4,128)} %param.21) | copy-start | bytes 3076
  22.9 0.7 copy-start
  24.1 11.1 %collective-permute-start.1 = (bf16[64,2048]{1,0:T(8,128)(2,1)S(1)}, bf16[64,2048]{1,0:T(8,128)(2,1)S(1)}, u32[]{:S(2)}, u32[]{:S(2)}) collective-permute-start(bf16[64,2048]{1,0:T(8,128)(2,1)S(1)} %collective-permute-done.q_ref), channel_id=1, source_target_pairs={{0,2},{2,4},{4,6},{6,0},{1,3},{3,5},{5,7},{7,1},{8,10},{10,12},{12... | collective-permute-start | bytes 786440 | tf_op jit(solution)/shard_map/ppermute | solution.py:272
  35.3 13.4 %collective-permute-start.3 = (bf16[64,2048]{1,0:T(8,128)(2,1)S(1)}, bf16[64,2048]{1,0:T(8,128)(2,1)S(1)}, u32[]{:S(2)}, u32[]{:S(2)}) collective-permute-start(bf16[64,2048]{1,0:T(8,128)(2,1)S(1)} %collective-permute-done.1.q_ref), channel_id=1, source_target_pairs={{0,2},{2,4},{4,6},{6,0},{1,3},{3,5},{5,7},{7,1},{8,10},{10,12},{12... | collective-permute-start | bytes 786440 | tf_op jit(solution)/shard_map/ppermute | solution.py:272
  36.9 23.2 %collective-permute-start.2 = (bf16[64,2176]{1,0:T(8,128)(2,1)S(1)}, bf16[64,2176]{1,0:T(8,128)(2,1)}, u32[]{:S(2)}, u32[]{:S(2)}) collective-permute-start(bf16[64,2176]{1,0:T(8,128)(2,1)S(1)} %attend.5), channel_id=1, source_target_pairs={{0,6},{2,0},{4,2},{6,4},{1,7},{3,1},{5,3},{7,5},{8,14},{10,8},{12,... | collective-permute-start | bytes 835592 | tf_op jit(solution)/shard_map/ppermute | solution.py:272
  58.3 11.4 %collective-permute-start.5 = (bf16[64,2176]{1,0:T(8,128)(2,1)S(1)}, bf16[64,2176]{1,0:T(8,128)(2,1)S(1)}, u32[]{:S(2)}, u32[]{:S(2)}) collective-permute-start(bf16[64,2176]{1,0:T(8,128)(2,1)S(1)} %attend.7), channel_id=1, source_target_pairs={{0,2},{2,4},{4,6},{6,0},{1,3},{3,5},{5,7},{7,1},{8,10},{10,12},{12... | collective-permute-start | bytes 835592 | tf_op jit(solution)/shard_map/ppermute | solution.py:272
  58.3 20.2 %collective-permute-start.4 = (bf16[64,2176]{1,0:T(8,128)(2,1)S(1)}, bf16[64,2176]{1,0:T(8,128)(2,1)S(1)}, u32[]{:S(2)}, u32[]{:S(2)}) collective-permute-start(bf16[64,2176]{1,0:T(8,128)(2,1)S(1)} %attend.6), channel_id=1, source_target_pairs={{0,4},{2,6},{4,0},{6,2},{1,5},{3,7},{5,1},{7,3},{8,12},{10,14},{12... | collective-permute-start | bytes 835592 | tf_op jit(solution)/shard_map/ppermute | solution.py:272
  69.7 8.8 %copy-start.5 = (bf16[64,2176]{1,0:T(8,128)(2,1)}, bf16[64,2176]{1,0:T(8,128)(2,1)S(1)}, u32[]{:S(2)}) copy-start(bf16[64,2176]{1,0:T(8,128)(2,1)S(1)} %collective-permute-done.5.refs_3_) | copy-start | bytes 835588
  78.5 0.7 copy-start.6
  79.2 19.1 %copy-start.4 = (bf16[1,64,2880]{2,1,0:T(8,128)(2,1)S(1)}, bf16[1,64,2880]{2,1,0:T(8,128)(2,1)}, u32[]{:S(2)}) copy-start(bf16[1,64,2880]{2,1,0:T(8,128)(2,1)} %param.13) | copy-start | bytes 1105924
  88.3 11.4 %copy-start.9 = (f32[2880]{0:T(1024)S(1)}, f32[2880]{0:T(1024)}, u32[]{:S(2)}) copy-start(f32[2880]{0:T(1024)} %param.20) | copy-start | bytes 34564
  88.3 10.1 %collective-permute-start.6 = (bf16[64,2880]{1,0:T(8,128)(2,1)}, bf16[64,2880]{1,0:T(8,128)(2,1)S(1)}, u32[]{:S(2)}, u32[]{:S(2)}) collective-permute-start(bf16[64,2880]{1,0:T(8,128)(2,1)} %merge_project.1), channel_id=1, source_target_pairs={{0,1},{1,0},{2,3},{3,2},{4,5},{5,4},{6,7},{7,6},{8,9},{9,8},{10,11... | collective-permute-start | bytes 1105928 | tf_op jit(solution)/shard_map/ppermute | solution.py:272
  157.3 3.3 %copy-start.11 = (f32[1,64,4]{1,2,0:T(4,128)S(1)}, f32[1,64,4]{1,2,0:T(4,128)}, u32[]{:S(2)}) copy-start(f32[1,64,4]{1,2,0:T(4,128)} %param.22) | copy-start | bytes 3076
  157.3 39.1 %all-to-all-start.1 = ((bf16[32,16,1440]{2,1,0:T(8,128)(2,1)}), bf16[32,16,1440]{2,1,0:T(8,128)(2,1)S(1)}, u32[]{:S(2)}, u32[]{:S(2)}) async-start(bf16[32,16,1440]{2,1,0:T(8,128)(2,1)} %bitcast.74), calls=%async_computation.1 | async-start | bytes 3145728 | tf_op jit(solution)/shard_map/all_to_all | solution.py:337

commit v2 on v1

--- a/solution.py
+++ b/solution.py
@@ -138,50 +138,48 @@
     tokens = packets[0].shape[0]
     width = packets[0].shape[1] - LANES
 
-    @pl.when(pl.program_id(0) == 0)
-    def _():
-        logs = []
-        for packet in packets:
-            pieces = packet[:, width:].astype(jnp.float32)
-            logs.append(pieces + (pltpu.roll(pieces, LANES - group, 1) + pltpu.roll(pieces, LANES - 2 * group, 1)))
-        top = functools.reduce(jnp.maximum, logs)
-        shares = [jnp.exp2(log - top) for log in logs]
-        total = functools.reduce(jnp.add, shares)
-        split = []
-        for share in shares:
-            share = share / total
-            coarse = share.astype(jnp.bfloat16)
-            split.append(jnp.concatenate([coarse, (share - coarse.astype(jnp.float32)).astype(jnp.bfloat16)], axis=1))
-        split = jnp.concatenate(split, axis=0)
-        half = LANES // 2
-        lanes = 2 * LANES
-        row = lax.broadcasted_iota(jnp.int32, (lanes, lanes), 0) % LANES
-        col = lax.broadcasted_iota(jnp.int32, (lanes, lanes), 1)
-        for start in range(0, width, lanes):
-            head = (col + start) // LANES + col % LANES // half * half
-            spread = jnp.where(row == head, 1.0, 0.0).astype(jnp.bfloat16)
-            wide = jnp.dot(split, spread, preferred_element_type=jnp.float32)
-            attn = 0.0
-            for i, packet in enumerate(packets):
-                attn = attn + wide[i * tokens:(i + 1) * tokens] * packet[:, start:start + lanes].astype(jnp.float32)
-            attn_ref[:, start:start + lanes] = attn.astype(jnp.bfloat16)
-
-    part = lax.dot_general(weight_ref[...], attn_ref[...], TURNED, preferred_element_type=jnp.float32)
-    out_ref[...] = part.T.astype(out_ref.dtype)
-
-
-def merge_project(packets, weight, group, block=5 * LANES):
+    logs = []
+    for packet in packets:
+        pieces = packet[:, width:].astype(jnp.float32)
+        logs.append(pieces + (pltpu.roll(pieces, LANES - group, 1) + pltpu.roll(pieces, LANES - 2 * group, 1)))
+    top = functools.reduce(jnp.maximum, logs)
+    shares = [jnp.exp2(log - top) for log in logs]
+    total = functools.reduce(jnp.add, shares)
+    split = []
+    for share in shares:
+        share = share / total
+        coarse = share.astype(jnp.bfloat16)
+        split.append(jnp.concatenate([coarse, (share - coarse.astype(jnp.float32)).astype(jnp.bfloat16)], axis=1))
+    split = jnp.concatenate(split, axis=0)
+    half = LANES // 2
+    lanes = 2 * LANES
+    row = lax.broadcasted_iota(jnp.int32, (lanes, lanes), 0) % LANES
+    col = lax.broadcasted_iota(jnp.int32, (lanes, lanes), 1)
+    for start in range(0, width, lanes):
+        head = (col + start) // LANES + col % LANES // half * half
+        spread = jnp.where(row == head, 1.0, 0.0).astype(jnp.bfloat16)
+        wide = jnp.dot(split, spread, preferred_element_type=jnp.float32)
+        attn = 0.0
+        for i, packet in enumerate(packets):
+            attn = attn + wide[i * tokens:(i + 1) * tokens] * packet[:, start:start + lanes].astype(jnp.float32)
+        attn_ref[:, start:start + lanes] = attn.astype(jnp.bfloat16)
+
+    for start, stop in steps_of(weight_ref.shape[0], 5 * LANES):
+        part = lax.dot_general(weight_ref[start:stop], attn_ref[...], TURNED, preferred_element_type=jnp.float32)
+        out_ref[:, start:stop] = part.T.astype(out_ref.dtype)
+
+
+def merge_project(packets, weight, group):
     tokens = packets[0].shape[0]
     model, depth = weight.shape
     vm = pl.BlockSpec(memory_space=pltpu.VMEM)
     return pl.pallas_call(
         functools.partial(merge_kernel, count=len(packets), group=group),
         out_shape=jax.ShapeDtypeStruct((tokens, model), jnp.bfloat16),
-        grid=(pl.cdiv(model, block),),
-        in_specs=[vm] * len(packets) + [pl.BlockSpec((block, depth), lambda k: (k, 0))],
-        out_specs=pl.BlockSpec((tokens, block), lambda k: (0, k)),
+        in_specs=[vm] * (len(packets) + 1),
+        out_specs=vm,
         scratch_shapes=[pltpu.VMEM((tokens, depth), jnp.bfloat16)],
-        compiler_params=pltpu.CompilerParams(vmem_limit_bytes=58 * 1024 * 1024),
+        compiler_params=pltpu.CompilerParams(vmem_limit_bytes=12 * 1024 * 1024),
         cost_estimate=pl.CostEstimate(flops=2 * tokens * depth * model, bytes_accessed=2 * depth * model, transcendentals=0),
         name="merge_project",
     )(*packets, weight)
@@ -194,77 +192,211 @@
 TURNED = (((1,), (1,)), ((), ()))
 
 
-def expert_kernel(rows_ref, gate_hbm, up_hbm, down_hbm, out_ref, gate_ref, up_ref, down_ref, act_ref, acc_ref, sems, *, step):
-    hidden, model = gate_hbm.shape
+def fetch_kernel(*refs, count, step):
+    sources, targets, sems = refs[:count], refs[count + 1:2 * count + 1], refs[2 * count + 1]
     pairs = []
-    for start, stop in steps_of(hidden, step):
-        pairs.append((gate_hbm.at[start:stop], gate_ref.at[start:stop]))
-        pairs.append((up_hbm.at[start:stop], up_ref.at[start:stop]))
-    later = len(pairs)
-    for start, stop in steps_of(hidden, step):
-        pairs.append((down_hbm.at[start:stop], down_ref.at[start:stop]))
+    for source, target in zip(sources, targets):
+        for start, stop in steps_of(source.shape[0], step):
+            pairs.append((source.at[start:stop], target.at[start:stop]))
     copies = [pltpu.make_async_copy(source, target, sems.at[i]) for i, (source, target) in enumerate(pairs)]
     for copy in copies:
         copy.start()
+    for copy in copies:
+        copy.wait()
+
+
+def fetch(arrays, after, step=3 * LANES):
+    stay = pl.BlockSpec(memory_space=pl.ANY)
+    number = sum(pl.cdiv(array.shape[0], step) for array in arrays)
+    size = sum(2 * array.size for array in arrays)
+    return pl.pallas_call(
+        functools.partial(fetch_kernel, count=len(arrays), step=step),
+        out_shape=[pltpu.VMEM(array.shape, array.dtype) for array in arrays],
+        in_specs=[stay] * (len(arrays) + 1),
+        out_specs=[pl.BlockSpec(memory_space=pltpu.VMEM)] * len(arrays),
+        scratch_shapes=[pltpu.SemaphoreType.DMA((number,))],
+        compiler_params=pltpu.CompilerParams(vmem_limit_bytes=1024 * 1024),
+        cost_estimate=pl.CostEstimate(flops=size, bytes_accessed=size, transcendentals=0),
+        name="fetch",
+    )(*[pltpu.with_memory_space_constraint(array, pltpu.HBM) for array in arrays], after)
+
+
+def expert_kernel(part_ref, *refs, count, step, pieces):
+    blocks, (gate_ref, up_ref, down_ref), rest = refs[:count], refs[count:count + 3], refs[count + 3:]
+    out_refs, (rows_ref, act_ref, acc_ref) = rest[:-3], rest[-3:]
+    hidden, model = gate_ref.shape
+    size = blocks[0].shape[0]
+    for j, block in enumerate(blocks):
+        rows_ref[j * size:(j + 1) * size] = block[...]
     rows = rows_ref[...]
-    for i, (start, stop) in enumerate(steps_of(hidden, step)):
-        copies[2 * i].wait()
-        copies[2 * i + 1].wait()
+    for start, stop in steps_of(hidden, step):
         gate = lax.dot_general(gate_ref[start:stop], rows, TURNED, preferred_element_type=jnp.float32)
         up = lax.dot_general(up_ref[start:stop], rows, TURNED, preferred_element_type=jnp.float32)
         act = gate * jax.nn.sigmoid(1.702 * gate) * (up + 1.0)
         act_ref[:, start:stop] = act.T.astype(jnp.bfloat16)
-    for copy in copies[later:]:
-        copy.wait()
     act = act_ref[...]
     for start, stop in steps_of(model, 4 * LANES):
         acc_ref[:, start:stop] = jnp.dot(act, down_ref[:, start:stop], preferred_element_type=jnp.float32)
-    width = out_ref.shape[2]
-    for i in range(out_ref.shape[0]):
-        out_ref[i] = acc_ref[:, i * width:(i + 1) * width].astype(out_ref.dtype)
-
-
-def expert(rows, gate, up, down, pieces, step=2 * LANES):
-    count, model = rows.shape
+    chunks = len(out_refs) // pieces
+    width = out_refs[0].shape[1]
+    for shift in range(pieces):
+        for i in range(pieces):
+
+            @pl.when(part_ref[0] == (i - shift) % pieces)
+            def _():
+                start = 0
+                for out_ref in out_refs[shift * chunks:(shift + 1) * chunks]:
+                    stop = start + out_ref.shape[0]
+                    out_ref[...] = acc_ref[start:stop, i * width:(i + 1) * width].astype(out_ref.dtype)
+                    start = stop
+
+
+def expert(part, blocks, gate, up, down, pieces, sizes, step=4 * LANES):
+    size, model = blocks[0].shape
+    count = size * len(blocks)
     hidden = gate.shape[0]
     vm = pl.BlockSpec(memory_space=pltpu.VMEM)
-    stay = pl.BlockSpec(memory_space=pl.ANY)
-    return pl.pallas_call(
-        functools.partial(expert_kernel, step=step),
-        out_shape=jax.ShapeDtypeStruct((pieces, count, model // pieces), jnp.bfloat16),
-        in_specs=[vm] + [stay] * 3,
+    return pl.pallas_call(
+        functools.partial(expert_kernel, count=len(blocks), step=step, pieces=pieces),
+        out_shape=[jax.ShapeDtypeStruct((n * size, model // pieces), jnp.bfloat16) for _ in range(pieces) for n in sizes],
+        in_specs=[pl.BlockSpec(memory_space=pltpu.SMEM)] + [vm] * (len(blocks) + 3),
+        out_specs=[vm] * (pieces * len(sizes)),
+        scratch_shapes=[
+            pltpu.VMEM((count, model), jnp.bfloat16),
+            pltpu.VMEM((count, hidden), jnp.bfloat16),
+            pltpu.VMEM((count, model), jnp.float32),
+        ],
+        compiler_params=pltpu.CompilerParams(vmem_limit_bytes=20 * 1024 * 1024),
+        cost_estimate=pl.CostEstimate(flops=6 * count * model * hidden, bytes_accessed=6 * model * hidden, transcendentals=0),
+        name="expert",
+    )(part.astype(jnp.int32).reshape(1), *blocks, gate, up, down)
+
+
+def gather_kernel(*refs, count):
+    total = refs[0][...].astype(jnp.float32)
+    for ref in refs[1:count]:
+        total = total + ref[...].astype(jnp.float32)
+    total = total.astype(jnp.bfloat16)
+    for j, out_ref in enumerate(refs[count:]):
+        out_ref[...] = total[j * CAP:(j + 1) * CAP]
+
+
+def gather_parts(parts):
+    rows, width = parts[0].shape
+    vm = pl.BlockSpec(memory_space=pltpu.VMEM)
+    return pl.pallas_call(
+        functools.partial(gather_kernel, count=len(parts)),
+        out_shape=[jax.ShapeDtypeStruct((CAP, width), jnp.bfloat16)] * (rows // CAP),
+        in_specs=[vm] * len(parts),
+        out_specs=[vm] * (rows // CAP),
+        compiler_params=pltpu.CompilerParams(vmem_limit_bytes=8 * 1024 * 1024),
+        cost_estimate=pl.CostEstimate(flops=rows * width * len(parts), bytes_accessed=2 * rows * width, transcendentals=0),
+        name="gather_parts",
+    )(*parts)
+
+
+def portions(total):
+    cuts = [total * k // 16 for k in (0, 3, 7, 12, 16)]
+    return [b - a for a, b in zip(cuts, cuts[1:])]
+
+
+def pack_kernel(tokens_ref, parts_refs, gain_ref, select_ref, resid_ref, *out_refs):
+    resid = tokens_ref[...].astype(jnp.float32)
+    for part_ref in parts_refs:
+        resid = resid + part_ref[...].astype(jnp.float32)
+    scale = lax.rsqrt(jnp.mean(resid * resid, axis=-1, keepdims=True) + 1e-05)
+    resid_ref[...] = resid
+    normed = (resid * scale * gain_ref[...]).astype(jnp.bfloat16)
+    for start, stop in steps_of(normed.shape[1], 4 * LANES):
+        piece = jnp.dot(select_ref[...], normed[:, start:stop], preferred_element_type=jnp.float32)
+        for j, out_ref in enumerate(out_refs):
+            out_ref[:, start:stop] = piece[j * CAP:(j + 1) * CAP].astype(jnp.bfloat16)
+
+
+def pack(tokens, parts, gain, select):
+    count, model = tokens.shape
+    vm = pl.BlockSpec(memory_space=pltpu.VMEM)
+    slots = select.shape[0]
+
+    def whole(*refs):
+        tokens_ref, parts, rest = refs[0], refs[1:1 + number], refs[1 + number:]
+        pack_kernel(tokens_ref, parts, *rest)
+
+    number = len(parts)
+    return pl.pallas_call(
+        whole,
+        out_shape=[jax.ShapeDtypeStruct((count, model), jnp.float32)]
+        + [jax.ShapeDtypeStruct((CAP, model), jnp.bfloat16)] * (slots // CAP),
+        in_specs=[vm] * (3 + number),
+        out_specs=[vm] * (1 + slots // CAP),
+        compiler_params=pltpu.CompilerParams(vmem_limit_bytes=16 * 1024 * 1024),
+        cost_estimate=pl.CostEstimate(flops=2 * slots * count * model, bytes_accessed=2 * slots * model, transcendentals=0),
+        name="pack",
+    )(tokens, *parts, gain.reshape(1, model), select)
+
+
+def project_kernel(x_ref, weight_hbm, out_ref, weight_ref, acc_ref, sems, *, step):
+    cuts = steps_of(weight_hbm.shape[0], step)
+    copies = [pltpu.make_async_copy(weight_hbm.at[start:stop], weight_ref.at[start:stop], sems.at[i]) for i, (start, stop) in enumerate(cuts)]
+    for copy in copies:
+        copy.start()
+    for i, (start, stop) in enumerate(cuts):
+        copies[i].wait()
+        part = jnp.dot(x_ref[:, start:stop], weight_ref[start:stop], preferred_element_type=jnp.float32)
+        if i == 0:
+            acc_ref[...] = part
+        else:
+            acc_ref[...] += part
+    out_ref[...] = acc_ref[...].astype(out_ref.dtype)
+
+
+def project(x, weight, step=2 * LANES):
+    tokens, model = x.shape
+    width = weight.shape[1]
+    vm = pl.BlockSpec(memory_space=pltpu.VMEM)
+    return pl.pallas_call(
+        functools.partial(project_kernel, step=step),
+        out_shape=jax.ShapeDtypeStruct((tokens, width), jnp.bfloat16),
+        in_specs=[vm, pl.BlockSpec(memory_space=pl.ANY)],
         out_specs=vm,
         scratch_shapes=[
-            pltpu.VMEM((hidden, model), jnp.bfloat16),
-            pltpu.VMEM((hidden, model), jnp.bfloat16),
-            pltpu.VMEM((hidden, model), jnp.bfloat16),
-            pltpu.VMEM((count, hidden), jnp.bfloat16),
-            pltpu.VMEM((count, model), jnp.float32),
-            pltpu.SemaphoreType.DMA((3 * pl.cdiv(hidden, step),)),
+            pltpu.VMEM((model, width), jnp.bfloat16),
+            pltpu.VMEM((tokens, width), jnp.float32),
+            pltpu.SemaphoreType.DMA((pl.cdiv(model, step),)),
         ],
         compiler_params=pltpu.CompilerParams(vmem_limit_bytes=56 * 1024 * 1024),
-        cost_estimate=pl.CostEstimate(flops=6 * count * model * hidden, bytes_accessed=6 * model * hidden, transcendentals=0),
-        name="expert",
-    )(rows, gate, up, down)
-
-
-def project_kernel(x_ref, weight_ref, out_ref):
-    out_ref[...] = jnp.dot(x_ref[...], weight_ref[...], preferred_element_type=jnp.float32).astype(out_ref.dtype)
-
-
-def project(x, weight, block=2 * LANES):
-    tokens, model = x.shape
-    width = weight.shape[1]
-    return pl.pallas_call(
-        project_kernel,
-        out_shape=jax.ShapeDtypeStruct((tokens, width), jnp.bfloat16),
-        grid=(pl.cdiv(width, block),),
-        in_specs=[pl.BlockSpec((tokens, model), lambda n: (0, 0)), pl.BlockSpec((model, block), lambda n: (0, n))],
-        out_specs=pl.BlockSpec((tokens, block), lambda n: (0, n)),
-        compiler_params=pltpu.CompilerParams(vmem_limit_bytes=58 * 1024 * 1024),
         cost_estimate=pl.CostEstimate(flops=2 * tokens * model * width, bytes_accessed=2 * model * width, transcendentals=0),
         name="project",
     )(x, weight)
+
+
+def combine_kernel(spread_ref, resid_ref, *refs):
+    parts_ref, out_ref = refs[-1], refs[-2]
+    for j, ref in enumerate(refs[:-2]):
+        parts_ref[j * CAP:(j + 1) * CAP] = ref[...]
+    spread = spread_ref[...]
+    parts = parts_ref[...]
+    total = resid_ref[...]
+    for _ in range(3):
+        coarse = spread.astype(jnp.bfloat16)
+        spread = spread - coarse.astype(jnp.float32)
+        total = total + jnp.dot(coarse, parts, preferred_element_type=jnp.float32)
+    out_ref[...] = total.astype(out_ref.dtype)
+
+
+def combine(spread, parts, resid):
+    vm = pl.BlockSpec(memory_space=pltpu.VMEM)
+    count, width = resid.shape
+    return pl.pallas_call(
+        combine_kernel,
+        out_shape=jax.ShapeDtypeStruct((count, width), jnp.bfloat16),
+        in_specs=[vm] * (2 + len(parts)),
+        out_specs=vm,
+        scratch_shapes=[pltpu.VMEM((spread.shape[1], width), jnp.bfloat16)],
+        compiler_params=pltpu.CompilerParams(vmem_limit_bytes=16 * 1024 * 1024),
+        cost_estimate=pl.CostEstimate(flops=6 * count * width * spread.shape[1], bytes_accessed=2 * width * spread.shape[1], transcendentals=0),
+        name="combine",
+    )(spread, resid, *parts)
 
 
 def shifted(block, axis, distance):
@@ -307,43 +439,50 @@
     for d in range(cycles):
         following = shifted(block, "ctx", 1) if d < cycles - 1 else None
         packet = attend(place, (place - d) % cycles, block, keys, values, fresh_keys, fresh_values)
+        kept = packet
         if d < cycles - 1:
             following, packet = lax.optimization_barrier((following, packet))
         packets.append(packet if d == 0 else shifted(packet, "ctx", -d))
         block = following
     group = query.shape[1] // LANES
-    projected = merge_project(packets, out_weight.T, group)
-    resid = tokens.astype(jnp.float32) + projected.astype(jnp.float32)
+    (mixing,) = fetch([out_weight.T], kept)
+    projected = merge_project(packets, mixing, group)
+    parts = [projected]
     for d in range(1, heads):
-        resid = resid + shifted(projected, "head", d).astype(jnp.float32)
+        parts.append(shifted(projected, "head", d))
     width = model // heads
-    resid_own = lax.dynamic_slice_in_dim(resid, lax.axis_index("head") * width, width, 1)
-    normed = (
-        resid * lax.rsqrt(jnp.mean(resid * resid, axis=-1, keepdims=True) + 1e-05) * norm_gain
-    ).astype(jnp.bfloat16)
     experts = lax.axis_size("seq") * lax.axis_size("ctx")
     slots = experts * CAP
     chosen = expert_ids[0].reshape(-1)
     onehot = (chosen[:, None] == lax.broadcasted_iota(jnp.int32, (1, experts), 1)).astype(jnp.int32)
     before = jnp.cumsum(onehot, axis=0) - onehot
-    target = chosen * CAP + jnp.sum(before * onehot, axis=1)
-    matches = target[None, :] == lax.broadcasted_iota(jnp.int32, (slots, 1), 0)
-    select = jnp.sum(matches.astype(jnp.float32).reshape(slots, count, -1), axis=-1).astype(jnp.bfloat16)
-    packed = jnp.dot(select, normed, preferred_element_type=jnp.float32).astype(jnp.bfloat16)
-    packed = packed.reshape(experts, CAP, model)
-    arrived = lax.all_to_all(packed, ("seq", "ctx"), split_axis=0, concat_axis=0, tiled=True)
-    parts = expert(arrived.reshape(slots, model), gate_weight[0].T, up_weight[0].T, down_weight[0], heads)
-    parts = parts.reshape(heads * experts, CAP, width)
-    returned = lax.all_to_all(parts, ("head", "seq", "ctx"), split_axis=0, concat_axis=0, tiled=True)
-    spread = jnp.where(matches.T, expert_weights[0].reshape(-1)[:, None], 0.0)
+    slot = jnp.sum(before * onehot, axis=1)
+    own = (lax.axis_index("seq") * cycles + place).astype(jnp.int32)
+    ahead = ((chosen - own) % experts * CAP + slot)[None, :] == lax.broadcasted_iota(jnp.int32, (slots, 1), 0)
+    select = jnp.sum(ahead.astype(jnp.float32).reshape(slots, count, -1), axis=-1).astype(jnp.bfloat16)
+    resid, *packed = pack(tokens, parts, norm_gain, select)
+    resid_own = lax.dynamic_slice_in_dim(resid, lax.axis_index("head") * width, width, 1)
+    arrived = [packed[0]]
+    for j in range(1, experts):
+        arrived.append(shifted(packed[j], ("seq", "ctx"), j))
+    fetched = fetch([gate_weight[0].T, up_weight[0].T, down_weight[0]], packed[0])
+    sizes = portions(experts)
+    pieces = expert(lax.axis_index("head"), arrived[1:] + arrived[:1], *fetched, heads, sizes)
+    crossed = []
+    for k in range(len(sizes)):
+        crossed.append([pieces[k]])
+        for d in range(1, heads):
+            crossed[k].append(shifted(pieces[d * len(sizes) + k], "head", d))
+    returned, j = {}, 1
+    for k in range(len(sizes)):
+        gathered = gather_parts(crossed[k])
+        for block in gathered:
+            returned[j % experts] = shifted(block, ("seq", "ctx"), -j) if j < experts else block
+            j += 1
+    spread = jnp.where(ahead.T, expert_weights[0].reshape(-1)[:, None], 0.0)
     spread = jnp.sum(spread.reshape(count, -1, slots), axis=1)
-    moe = lax.dot_general(
-        jnp.tile(spread, (1, heads)),
-        returned.reshape(heads * slots, width).astype(jnp.float32),
-        (((1,), (0,)), ((), ())),
-        precision=lax.Precision.HIGHEST,
-    )
-    return (resid_own + moe).astype(jnp.bfloat16)[None]
+    mixed = combine(spread, [returned[j] for j in range(experts)], resid_own)
+    return mixed[None]
 
 
 def solution(mesh):

time: 200 us -> 175 us (0.88); the launches traced: 198 us -> 175 us
  starting transfers between devices: 14.4 us -> 60.2 us
  blocking collectives: 40 us -> 0 us
  waiting for transfers between devices: 62.1 us -> 38.6 us
  matrix products: 3.41 us -> 0 us
  local copies, waits for them, and re-layouts: 5.2 us -> 2.2 us
  Pallas kernels: 70.1 us -> 72.6 us
    ppermute x7 -> x41, starting transfers between devices: 11.1 us -> 60.2 us  [shifted(): lax.ppermute(block, axis, [(i, (i + distance) % size) for i in range(size)])]
    all_to_all x1 -> x0, blocking collectives: 40 us -> none  [body(): lax.all_to_all(packed, ('seq', 'ctx'), split_axis=0, concat_axis=0, tiled...]
    all_to_all x1 -> x0, waiting for transfers between devices: 35.6 us -> none  [body(): lax.all_to_all(parts, ('head', 'seq', 'ctx'), split_axis=0, concat_axis=0...]
    ppermute x7 -> x41, waiting for transfers between devices: 26.5 us -> 38.6 us  [shifted(): lax.ppermute(block, axis, [(i, (i + distance) % size) for i in range(size)])]
    pallas_call x2 -> x10, Pallas kernels: 22.8 us -> 29.3 us  [the longest x2 12.8 us: fetch(): pl.pallas_call(functools.partial(fetch_kernel, count=len(arrays), step=st...]
    pallas_call x1, Pallas kernels: 9.07 us -> 3.67 us  [merge_project(): pl.pallas_call(functools.partial(merge_kernel, count=len(packets), group=...]
    dot_general x2 -> x0, matrix products: 3.41 us -> none  [the longest x1 1.82 us: body(): jnp.dot(select, normed, preferred_element_type=jnp.float32)]
    all_to_all x1 -> x0, starting transfers between devices: 3.3 us -> none  [body(): lax.all_to_all(parts, ('head', 'seq', 'ctx'), split_axis=0, concat_axis=0...]
  transfers between devices with their start and end apart: 8 -> 41, of which waited for: 4 -> 11; matrix products, arithmetic and copies ran while one was open for 1% -> 1% of each run, Pallas kernels for 19% -> 30%
where the time goes in v2:
time: 175 us
  Pallas kernels  72.6 us (41%)
  starting transfers between devices  60.2 us (34%)
  waiting for transfers between devices  38.6 us (22%)
  local copies, waits for them, and re-layouts  2.2 us (1%)
    ppermute x41, starting transfers between devices, shifted(): lax.ppermute(block, axis, [(i, (i + distance) % size) for i in range(size)])  60.2 us
    pallas_call x4, Pallas kernels, attend(): pl.pallas_call(functools.partial(attend_kernel, tokens=tokens, kv=kv, pai...  39.6 us
    ppermute x41, waiting for transfers between devices, shifted(): lax.ppermute(block, axis, [(i, (i + distance) % size) for i in range(size)])  38.6 us
    pallas_call x2, Pallas kernels, fetch(): pl.pallas_call(functools.partial(fetch_kernel, count=len(arrays), step=st...  12.8 us
    pallas_call x1, Pallas kernels, expert(): pl.pallas_call(functools.partial(expert_kernel, count=len(blocks), step=s...  7.57 us
    pallas_call x1, Pallas kernels, project(): pl.pallas_call(functools.partial(project_kernel, step=step), out_shape=ja...  6.63 us
    pallas_call x1, Pallas kernels, merge_project(): pl.pallas_call(functools.partial(merge_kernel, count=len(packets), group=...  3.67 us
  transfers between devices with their start and end apart: 41, of which 11 were waited for; matrix products, arithmetic and copies ran while one was open for 1% of the time, Pallas kernels for 30%

profile of v2, /device:TPU:0, one launch (start us, length us, event | category | flops | bytes accessed | tf_op | source)
XLA Modules:
  0.0 175.3 jit_solution(4757078545806167324)
XLA Ops:
  0.0 6.6 %project.1.q_ref = bf16[64,2048]{1,0:T(8,128)(2,1)} custom-call(bf16[64,2880]{1,0:T(8,128)(2,1)} %bitcast.52, bf16[2880,2048]{1,0:T(8,128)(2,1)} %weight_hbm.1), custom_call_target="tpu_custom_call" | custom-call | flops 754974720 | bytes 11796480 | tf_op jit(solution)/shard_map/project/pallas_call | solution.py:357
  6.6 3.1 %collective-permute-start = (bf16[64,2048]{1,0:T(8,128)(2,1)}, bf16[64,2048]{1,0:T(8,128)(2,1)S(1)}, u32[]{:S(2)}, u32[]{:S(2)}) collective-permute-start(bf16[64,2048]{1,0:T(8,128)(2,1)} %project.1.q_ref), channel_id=1, source_target_pairs={{0,2},{2,4},{4,6},{6,0},{1,3},{3,5},{5,7},{7,1},{8,10},{10,12},{12... | collective-permute-start | bytes 786440 | tf_op jit(solution)/shard_map/ppermute | solution.py:404
  10.2 0.9 copy-done.1
  11.1 9.5 %attend.4.refs_0_ = bf16[64,2176]{1,0:T(8,128)(2,1)S(1)} custom-call(s32[2]{0:T(128)S(1)} %pad_add_fusion.where_ref, bf16[64,2048]{1,0:T(8,128)(2,1)S(1)} %copy-done.1, bf16[4,64,2048]{2,1,0:T(8,128)(2,1)S(1)} %bitcast.54, bf16[4,64,2048]{2,1,0:T(8,128)(2,1)S(1)} %bitcast.58, bf16[4,64,128]{2,1,0:T(8,128)(2,1)S(1)} %pad.7.nk_ref, ...), custom_call_target="tpu_custom_call" | custom-call | flops 4563402752 | tf_op jit(solution)/shard_map/attend/pallas_call | solution.py:124
  21.2 1.6 collective-permute-start.1
  22.8 10.3 %attend.5 = bf16[64,2176]{1,0:T(8,128)(2,1)} custom-call(s32[2]{0:T(128)S(1)} %pad_add_fusion.1.where_ref, bf16[64,2048]{1,0:T(8,128)(2,1)S(1)} %collective-permute-done.q_ref, bf16[4,64,2048]{2,1,0:T(8,128)(2,1)S(1)} %bitcast.55, bf16[4,64,2048]{2,1,0:T(8,128)(2,1)S(1)} %bitcast.59, bf16[4,64,128]{2,1,0:T(8,128)(2,1)S(1)} %pad.7.nk_ref, ...), custom_call_target="tpu_custom_call" | custom-call | flops 4563402752 | tf_op jit(solution)/shard_map/attend/pallas_call | solution.py:124
  33.1 1.6 collective-permute-start.3
  34.7 2.2 %collective-permute-start.2 = (bf16[64,2176]{1,0:T(8,128)(2,1)}, bf16[64,2176]{1,0:T(8,128)(2,1)S(1)}, u32[]{:S(2)}, u32[]{:S(2)}) collective-permute-start(bf16[64,2176]{1,0:T(8,128)(2,1)} %attend.5), channel_id=1, source_target_pairs={{0,6},{2,0},{4,2},{6,4},{1,7},{3,1},{5,3},{7,5},{8,14},{10,8},{12,... | collective-permute-start | bytes 835592 | tf_op jit(solution)/shard_map/ppermute | solution.py:404
  36.9 10.3 %attend.6 = bf16[64,2176]{1,0:T(8,128)(2,1)} custom-call(s32[2]{0:T(128)S(1)} %pad_add_fusion.2.where_ref, bf16[64,2048]{1,0:T(8,128)(2,1)S(1)} %collective-permute-done.1.q_ref, bf16[4,64,2048]{2,1,0:T(8,128)(2,1)S(1)} %bitcast.56, bf16[4,64,2048]{2,1,0:T(8,128)(2,1)S(1)} %bitcast.60, bf16[4,64,128]{2,1,0:T(8,128)(2,1)S(1)} %pad.7.nk_ref, ...), custom_call_target="tpu_custom_call" | custom-call | flops 4563402752 | tf_op jit(solution)/shard_map/attend/pallas_call | solution.py:124
  47.2 9.5 %attend.7.refs_1_ = bf16[64,2176]{1,0:T(8,128)(2,1)S(1)} custom-call(s32[2]{0:T(128)S(1)} %pad_add_fusion.3.where_ref, bf16[64,2048]{1,0:T(8,128)(2,1)S(1)} %collective-permute-done.3.q_ref, bf16[4,64,2048]{2,1,0:T(8,128)(2,1)S(1)} %bitcast.57, bf16[4,64,2048]{2,1,0:T(8,128)(2,1)S(1)} %bitcast.61, bf16[4,64,128]{2,1,0:T(8,128)(2,1)S(1)} %pad.7.nk_ref, ...), custom_call_target="tpu_custom_call" | custom-call | flops 4563402752 | tf_op jit(solution)/shard_map/attend/pallas_call | solution.py:124
  56.8 1.0 collective-permute-start.4
  58.6 4.4 %fetch.2.refs_4_ = bf16[2880,2048]{1,0:T(8,128)(2,1)S(1)} custom-call(bf16[2880,2048]{1,0:T(8,128)(2,1)} %bitcast.62, bf16[64,2176]{1,0:T(8,128)(2,1)S(1)} %attend.7.refs_1_), custom_call_target="tpu_custom_call" | custom-call | flops 11796480 | bytes 11796480 | tf_op jit(solution)/shard_map/fetch/pallas_call | solution.py:212
  63.1 5.1 %collective-permute-done.5.refs_3_ = bf16[64,2176]{1,0:T(8,128)(2,1)S(1)} collective-permute-done((bf16[64,2176]{1,0:T(8,128)(2,1)S(1)}, bf16[64,2176]{1,0:T(8,128)(2,1)S(1)}, u32[]{:S(2)}, u32[]{:S(2)}) %collective-permute-start.5) | collective-permute-done | bytes 278560 | tf_op jit(solution)/shard_map/ppermute | solution.py:404
  68.2 9.0 %collective-permute-done.4.refs_2_ = bf16[64,2176]{1,0:T(8,128)(2,1)S(1)} collective-permute-done((bf16[64,2176]{1,0:T(8,128)(2,1)}, bf16[64,2176]{1,0:T(8,128)(2,1)S(1)}, u32[]{:S(2)}, u32[]{:S(2)}) %collective-permute-start.4) | collective-permute-done | bytes 278560 | tf_op jit(solution)/shard_map/ppermute | solution.py:404
  77.2 3.7 %merge_project.1.refs_1_ = bf16[64,2880]{1,0:T(8,128)(2,1)S(1)} custom-call(bf16[64,2176]{1,0:T(8,128)(2,1)S(1)} %attend.4.refs_0_, bf16[64,2176]{1,0:T(8,128)(2,1)S(1)} %collective-permute-done.2.refs_1_, bf16[64,2176]{1,0:T(8,128)(2,1)S(1)} %collective-permute-done.4.refs_2_, bf16[64,2176]{1,0:T(8,128)(2,1)S(1)} %collective-permute-done.5.refs_3_, ...), custom_call_target="tpu_custom_call" | custom-call | flops 754974720 | bytes 11796480 | tf_op jit(solution)/shard_map/merge_project/pallas_call | solution.py:176
  80.9 1.6 collective-permute-start.6
  83.0 8.0 %collective-permute-done.6.refs_2_ = bf16[64,2880]{1,0:T(8,128)(2,1)S(1)} collective-permute-done((bf16[64,2880]{1,0:T(8,128)(2,1)S(1)}, bf16[64,2880]{1,0:T(8,128)(2,1)S(1)}, u32[]{:S(2)}, u32[]{:S(2)}) %collective-permute-start.6) | collective-permute-done | bytes 368672 | tf_op jit(solution)/shard_map/ppermute | solution.py:404
  91.0 0.8 pack.1
  92.0 1.9 %collective-permute-start.9 = (bf16[16,2880]{1,0:T(8,128)(2,1)S(1)}, bf16[16,2880]{1,0:T(8,128)(2,1)S(1)}, u32[]{:S(2)}, u32[]{:S(2)}) collective-permute-start(bf16[16,2880]{1,0:T(8,128)(2,1)S(1)} %get-tuple-element.64), channel_id=1, source_target_pairs={{0,6},{2,8},{4,10},{6,12},{8,14},{10,16},{12,18},{14,20},{16,22},{... | collective-permute-start | bytes 276488 | tf_op jit(solution)/shard_map/ppermute | solution.py:404
  93.9 2.6 %collective-permute-start.10 = (bf16[16,2880]{1,0:T(8,128)(2,1)S(1)}, bf16[16,2880]{1,0:T(8,128)(2,1)S(1)}, u32[]{:S(2)}, u32[]{:S(2)}) collective-permute-start(bf16[16,2880]{1,0:T(8,128)(2,1)S(1)} %get-tuple-element.65), channel_id=1, source_target_pairs={{0,8},{2,10},{4,12},{6,14},{8,16},{10,18},{12,20},{14,22},{16,24},... | collective-permute-start | bytes 276488 | tf_op jit(solution)/shard_map/ppermute | solution.py:404
  96.6 3.0 %collective-permute-done.7.refs_0_ = bf16[16,2880]{1,0:T(8,128)(2,1)S(1)} collective-permute-done((bf16[16,2880]{1,0:T(8,128)(2,1)S(1)}, bf16[16,2880]{1,0:T(8,128)(2,1)S(1)}, u32[]{:S(2)}, u32[]{:S(2)}) %collective-permute-start.7) | collective-permute-done | bytes 92192 | tf_op jit(solution)/shard_map/ppermute | solution.py:404
  99.6 2.9 %collective-permute-done.8.refs_1_ = bf16[16,2880]{1,0:T(8,128)(2,1)S(1)} collective-permute-done((bf16[16,2880]{1,0:T(8,128)(2,1)S(1)}, bf16[16,2880]{1,0:T(8,128)(2,1)S(1)}, u32[]{:S(2)}, u32[]{:S(2)}) %collective-permute-start.8) | collective-permute-done | bytes 92192 | tf_op jit(solution)/shard_map/ppermute | solution.py:404
  102.5 0.7 collective-permute-start.13
  103.2 1.5 collective-permute-start.14
  104.7 5.9 %collective-permute-start.15 = (bf16[16,2880]{1,0:T(8,128)(2,1)S(1)}, bf16[16,2880]{1,0:T(8,128)(2,1)S(1)}, u32[]{:S(2)}, u32[]{:S(2)}) collective-permute-start(bf16[16,2880]{1,0:T(8,128)(2,1)S(1)} %get-tuple-element.70), channel_id=1, source_target_pairs={{0,18},{2,20},{4,22},{6,24},{8,26},{10,28},{12,30},{14,0},{16,2},{... | collective-permute-start | bytes 276488 | tf_op jit(solution)/shard_map/ppermute | solution.py:404
  110.6 1.9 %collective-permute-start.17 = (bf16[16,2880]{1,0:T(8,128)(2,1)S(1)}, bf16[16,2880]{1,0:T(8,128)(2,1)S(1)}, u32[]{:S(2)}, u32[]{:S(2)}) collective-permute-start(bf16[16,2880]{1,0:T(8,128)(2,1)S(1)} %get-tuple-element.72), channel_id=1, source_target_pairs={{0,22},{2,24},{4,26},{6,28},{8,30},{10,0},{12,2},{14,4},{16,6},{18... | collective-permute-start | bytes 276488 | tf_op jit(solution)/shard_map/ppermute | solution.py:404
  112.6 3.9 %collective-permute-start.19 = (bf16[16,2880]{1,0:T(8,128)(2,1)S(1)}, bf16[16,2880]{1,0:T(8,128)(2,1)S(1)}, u32[]{:S(2)}, u32[]{:S(2)}) collective-permute-start(bf16[16,2880]{1,0:T(8,128)(2,1)S(1)} %get-tuple-element.74), channel_id=1, source_target_pairs={{0,26},{2,28},{4,30},{6,0},{8,2},{10,4},{12,6},{14,8},{16,10},{18,... | collective-permute-start | bytes 276488 | tf_op jit(solution)/shard_map/ppermute | solution.py:404
  116.6 0.7 collective-permute-done.16.refs_9_
  117.3 1.4 collective-permute-start.21
  118.7 8.4 %fetch.3 = (bf16[1440,2880]{1,0:T(8,128)(2,1)S(1)}, bf16[1440,2880]{1,0:T(8,128)(2,1)S(1)}, bf16[1440,2880]{1,0:T(8,128)(2,1)S(1)}) custom-call(bf16[1440,2880]{1,0:T(8,128)(2,1)} %bitcast.63, bf16[1440,2880]{1,0:T(8,128)(2,1)} %bitcast.64, bf16[1440,2880]{1,0:T(8,128)(2,1)} %bitcast.65, bf16[16,2880]{1,0:T(8,128)(2,1)S(1)} %get-tuple-element.77.refs_3_.refs_15_), custom_call_target="tpu_custom_call" | custom-call | flops 24883200 | bytes 24883200 | tf_op jit(solution)/shard_map/fetch/pallas_call | solution.py:212
  127.2 7.6 %expert.1 = (bf16[48,1440]{1,0:T(8,128)(2,1)S(1)}, bf16[64,1440]{1,0:T(8,128)(2,1)S(1)}, bf16[80,1440]{1,0:T(8,128)(2,1)S(1)}, bf16[64,1440]{1,0:T(8,128)(2,1)S(...) custom-call(s32[1]{0:T(128)} %bitcast.20.part_ref, ...), custom_call_target="tpu_custom_call" | custom-call | flops 6370099200 | bytes 24883200 | tf_op jit(solution)/shard_map/expert/pallas_call | solution.py:259
  134.8 1.6 collective-permute-start.22
  136.9 1.5 collective-permute-start.27
  138.9 4.8 %collective-permute-done.23.refs_1_ = bf16[48,1440]{1,0:T(8,128)(2,1)S(1)} collective-permute-done((bf16[48,1440]{1,0:T(8,128)(2,1)S(1)}, bf16[48,1440]{1,0:T(8,128)(2,1)S(1)}, u32[]{:S(2)}, u32[]{:S(2)}) %collective-permute-start.23) | collective-permute-done | bytes 138272 | tf_op jit(solution)/shard_map/ppermute | solution.py:404
  143.7 3.3 %collective-permute-start.24 = (bf16[16,1440]{1,0:T(8,128)(2,1)S(1)}, bf16[16,1440]{1,0:T(8,128)(2,1)S(1)}, u32[]{:S(2)}, u32[]{:S(2)}) collective-permute-start(bf16[16,1440]{1,0:T(8,128)(2,1)S(1)} %get-tuple-element.86), channel_id=1, source_target_pairs={{0,30},{2,0},{4,2},{6,4},{8,6},{10,8},{12,10},{14,12},{16,14},{18,... | collective-permute-start | bytes 138248 | tf_op jit(solution)/shard_map/ppermute | solution.py:404
  147.0 2.3 %collective-permute-start.26 = (bf16[16,1440]{1,0:T(8,128)(2,1)S(1)}, bf16[16,1440]{1,0:T(8,128)(2,1)S(1)}, u32[]{:S(2)}, u32[]{:S(2)}) collective-permute-start(bf16[16,1440]{1,0:T(8,128)(2,1)S(1)} %get-tuple-element.88), channel_id=1, source_target_pairs={{0,26},{2,28},{4,30},{6,0},{8,2},{10,4},{12,6},{14,8},{16,10},{18,... | collective-permute-start | bytes 138248 | tf_op jit(solution)/shard_map/ppermute | solution.py:404
  149.4 4.8 %collective-permute-start.38 = (bf16[16,1440]{1,0:T(8,128)(2,1)S(1)}, bf16[16,1440]{1,0:T(8,128)(2,1)S(1)}, u32[]{:S(2)}, u32[]{:S(2)}) collective-permute-start(bf16[16,1440]{1,0:T(8,128)(2,1)S(1)} %get-tuple-element.102), channel_id=1, source_target_pairs={{0,6},{2,8},{4,10},{6,12},{8,14},{10,16},{12,18},{14,20},{16,22},{... | collective-permute-start | bytes 138248 | tf_op jit(solution)/shard_map/ppermute | solution.py:404
  154.9 2.9 %collective-permute-start.28 = (bf16[16,1440]{1,0:T(8,128)(2,1)S(1)}, bf16[16,1440]{1,0:T(8,128)(2,1)S(1)}, u32[]{:S(2)}, u32[]{:S(2)}) collective-permute-start(bf16[16,1440]{1,0:T(8,128)(2,1)S(1)} %get-tuple-element.91), channel_id=1, source_target_pairs={{0,24},{2,26},{4,28},{6,30},{8,0},{10,2},{12,4},{14,6},{16,8},{18,... | collective-permute-start | bytes 138248 | tf_op jit(solution)/shard_map/ppermute | solution.py:404
  157.8 2.7 %collective-permute-start.29 = (bf16[16,1440]{1,0:T(8,128)(2,1)S(1)}, bf16[16,1440]{1,0:T(8,128)(2,1)S(1)}, u32[]{:S(2)}, u32[]{:S(2)}) collective-permute-start(bf16[16,1440]{1,0:T(8,128)(2,1)S(1)} %get-tuple-element.92), channel_id=1, source_target_pairs={{0,22},{2,24},{4,26},{6,28},{8,30},{10,0},{12,2},{14,4},{16,6},{18... | collective-permute-start | bytes 138248 | tf_op jit(solution)/shard_map/ppermute | solution.py:404
  160.6 1.9 %collective-permute-start.31 = (bf16[16,1440]{1,0:T(8,128)(2,1)S(1)}, bf16[16,1440]{1,0:T(8,128)(2,1)S(1)}, u32[]{:S(2)}, u32[]{:S(2)}) collective-permute-start(bf16[16,1440]{1,0:T(8,128)(2,1)S(1)} %get-tuple-element.94), channel_id=1, source_target_pairs={{0,18},{2,20},{4,22},{6,24},{8,26},{10,28},{12,30},{14,0},{16,2},{... | collective-permute-start | bytes 138248 | tf_op jit(solution)/shard_map/ppermute | solution.py:404
  162.7 2.3 %collective-permute-start.33 = (bf16[16,1440]{1,0:T(8,128)(2,1)S(1)}, bf16[16,1440]{1,0:T(8,128)(2,1)S(1)}, u32[]{:S(2)}, u32[]{:S(2)}) collective-permute-start(bf16[16,1440]{1,0:T(8,128)(2,1)S(1)} %get-tuple-element.97), channel_id=1, source_target_pairs={{0,16},{2,18},{4,20},{6,22},{8,24},{10,26},{12,28},{14,30},{16,0},... | collective-permute-start | bytes 138248 | tf_op jit(solution)/shard_map/ppermute | solution.py:404
  165.0 0.9 collective-permute-start.34
  165.9 1.5 collective-permute-start.35
  167.3 0.9 collective-permute-start.36
  169.1 0.9 collective-permute-done.34.refs_9_
  170.0 2.8 %collective-permute-done.35.refs_10_ = bf16[16,1440]{1,0:T(8,128)(2,1)S(1)} collective-permute-done((bf16[16,1440]{1,0:T(8,128)(2,1)S(1)}, bf16[16,1440]{1,0:T(8,128)(2,1)S(1)}, u32[]{:S(2)}, u32[]{:S(2)}) %collective-permute-start.35) | collective-permute-done | bytes 46112 | tf_op jit(solution)/shard_map/ppermute | solution.py:404
  172.8 1.3 collective-permute-done.36.refs_11_
  174.1 1.2 combine.1
  (95 shorter events, 5.9 us)
Async XLA Ops:
  0.0 10.2 %copy-start.3 = (bf16[1,2048,4,64]{1,3,2,0:T(8,128)(2,1)S(1)}, bf16[1,2048,4,64]{1,3,2,0:T(8,128)(2,1)}, u32[]{:S(2)}) copy-start(bf16[1,2048,4,64]{1,3,2,0:T(8,128)(2,1)} %param.16) | copy-start | bytes 3145732
  0.0 10.2 %copy-start.2 = (bf16[1,2048,4,64]{1,3,2,0:T(8,128)(2,1)S(1)}, bf16[1,2048,4,64]{1,3,2,0:T(8,128)(2,1)}, u32[]{:S(2)}) copy-start(bf16[1,2048,4,64]{1,3,2,0:T(8,128)(2,1)} %param.15) | copy-start | bytes 3145732
  6.6 14.6 %collective-permute-start = (bf16[64,2048]{1,0:T(8,128)(2,1)}, bf16[64,2048]{1,0:T(8,128)(2,1)S(1)}, u32[]{:S(2)}, u32[]{:S(2)}) collective-permute-start(bf16[64,2048]{1,0:T(8,128)(2,1)} %project.1.q_ref), channel_id=1, source_target_pairs={{0,2},{2,4},{4,6},{6,0},{1,3},{3,5},{5,7},{7,1},{8,10},{10,12},{12... | collective-permute-start | bytes 786440 | tf_op jit(solution)/shard_map/ppermute | solution.py:404
  10.1 10.7 %copy-start.8 = (s32[1,64,4]{1,2,0:T(4,128)S(1)}, s32[1,64,4]{1,2,0:T(4,128)}, u32[]{:S(2)}) copy-start(s32[1,64,4]{1,2,0:T(4,128)} %param.21) | copy-start | bytes 3076
  21.2 11.8 %collective-permute-start.1 = (bf16[64,2048]{1,0:T(8,128)(2,1)S(1)}, bf16[64,2048]{1,0:T(8,128)(2,1)S(1)}, u32[]{:S(2)}, u32[]{:S(2)}) collective-permute-start(bf16[64,2048]{1,0:T(8,128)(2,1)S(1)} %collective-permute-done.q_ref), channel_id=1, source_target_pairs={{0,2},{2,4},{4,6},{6,0},{1,3},{3,5},{5,7},{7,1},{8,10},{10,12},{12... | collective-permute-start | bytes 786440 | tf_op jit(solution)/shard_map/ppermute | solution.py:404
  33.1 14.1 %collective-permute-start.3 = (bf16[64,2048]{1,0:T(8,128)(2,1)S(1)}, bf16[64,2048]{1,0:T(8,128)(2,1)S(1)}, u32[]{:S(2)}, u32[]{:S(2)}) collective-permute-start(bf16[64,2048]{1,0:T(8,128)(2,1)S(1)} %collective-permute-done.1.q_ref), channel_id=1, source_target_pairs={{0,2},{2,4},{4,6},{6,0},{1,3},{3,5},{5,7},{7,1},{8,10},{10,12},{12... | collective-permute-start | bytes 786440 | tf_op jit(solution)/shard_map/ppermute | solution.py:404
  34.7 28.4 %collective-permute-start.2 = (bf16[64,2176]{1,0:T(8,128)(2,1)}, bf16[64,2176]{1,0:T(8,128)(2,1)S(1)}, u32[]{:S(2)}, u32[]{:S(2)}) collective-permute-start(bf16[64,2176]{1,0:T(8,128)(2,1)} %attend.5), channel_id=1, source_target_pairs={{0,6},{2,0},{4,2},{6,4},{1,7},{3,1},{5,3},{7,5},{8,14},{10,8},{12,... | collective-permute-start | bytes 835592 | tf_op jit(solution)/shard_map/ppermute | solution.py:404
  56.7 11.4 %collective-permute-start.5 = (bf16[64,2176]{1,0:T(8,128)(2,1)S(1)}, bf16[64,2176]{1,0:T(8,128)(2,1)S(1)}, u32[]{:S(2)}, u32[]{:S(2)}) collective-permute-start(bf16[64,2176]{1,0:T(8,128)(2,1)S(1)} %attend.7.refs_1_), channel_id=1, source_target_pairs={{0,2},{2,4},{4,6},{6,0},{1,3},{3,5},{5,7},{7,1},{8,10},{10,12},{12... | collective-permute-start | bytes 835592 | tf_op jit(solution)/shard_map/ppermute | solution.py:404
  56.8 20.4 %collective-permute-start.4 = (bf16[64,2176]{1,0:T(8,128)(2,1)}, bf16[64,2176]{1,0:T(8,128)(2,1)S(1)}, u32[]{:S(2)}, u32[]{:S(2)}) collective-permute-start(bf16[64,2176]{1,0:T(8,128)(2,1)} %attend.6), channel_id=1, source_target_pairs={{0,4},{2,6},{4,0},{6,2},{1,5},{3,7},{5,1},{7,3},{8,12},{10,14},{12... | collective-permute-start | bytes 835592 | tf_op jit(solution)/shard_map/ppermute | solution.py:404
  63.0 19.5 %copy-start.6 = (f32[2880]{0:T(1024)S(1)}, f32[2880]{0:T(1024)}, u32[]{:S(2)}) copy-start(f32[2880]{0:T(1024)} %param.20) | copy-start | bytes 34564
  63.0 28.0 %copy-start = (bf16[1,64,2880]{2,1,0:T(8,128)(2,1)S(1)}, bf16[1,64,2880]{2,1,0:T(8,128)(2,1)}, u32[]{:S(2)}) copy-start(bf16[1,64,2880]{2,1,0:T(8,128)(2,1)} %param.13) | copy-start | bytes 1105924
  63.1 19.4 %slice-start = ((s32[16,3]{0,1:T(4,128)}), s32[16,2]{0,1:T(2,128)S(1)}, s32[]{:S(2)}) async-start(s32[16,3]{0,1:T(4,128)} %copy-done.7), calls=%async_computation | async-start | bytes 2048 | tf_op jit(solution)/shard_map/slice.1
  80.9 10.1 %collective-permute-start.6 = (bf16[64,2880]{1,0:T(8,128)(2,1)S(1)}, bf16[64,2880]{1,0:T(8,128)(2,1)S(1)}, u32[]{:S(2)}, u32[]{:S(2)}) collective-permute-start(bf16[64,2880]{1,0:T(8,128)(2,1)S(1)} %merge_project.1.refs_1_), channel_id=1, source_target_pairs={{0,1},{1,0},{2,3},{3,2},{4,5},{5,4},{6,7},{7,6},{8,9},{9,8},{10,11... | collective-permute-start | bytes 1105928 | tf_op jit(solution)/shard_map/ppermute | solution.py:404
  91.8 7.8 %collective-permute-start.7 = (bf16[16,2880]{1,0:T(8,128)(2,1)S(1)}, bf16[16,2880]{1,0:T(8,128)(2,1)S(1)}, u32[]{:S(2)}, u32[]{:S(2)}) collective-permute-start(bf16[16,2880]{1,0:T(8,128)(2,1)S(1)} %get-tuple-element.62), channel_id=1, source_target_pairs={{0,2},{2,4},{4,6},{6,8},{8,10},{10,12},{12,14},{14,16},{16,18},{18... | collective-permute-start | bytes 276488 | tf_op jit(solution)/shard_map/ppermute | solution.py:404
  91.9 10.6 %collective-permute-start.8 = (bf16[16,2880]{1,0:T(8,128)(2,1)S(1)}, bf16[16,2880]{1,0:T(8,128)(2,1)S(1)}, u32[]{:S(2)}, u32[]{:S(2)}) collective-permute-start(bf16[16,2880]{1,0:T(8,128)(2,1)S(1)} %get-tuple-element.63), channel_id=1, source_target_pairs={{0,4},{2,6},{4,8},{6,10},{8,12},{10,14},{12,16},{14,18},{16,20},{1... | collective-permute-start | bytes 276488 | tf_op jit(solution)/shard_map/ppermute | solution.py:404
  92.0 11.2 %collective-permute-start.9 = (bf16[16,2880]{1,0:T(8,128)(2,1)S(1)}, bf16[16,2880]{1,0:T(8,128)(2,1)S(1)}, u32[]{:S(2)}, u32[]{:S(2)}) collective-permute-start(bf16[16,2880]{1,0:T(8,128)(2,1)S(1)} %get-tuple-element.64), channel_id=1, source_target_pairs={{0,6},{2,8},{4,10},{6,12},{8,14},{10,16},{12,18},{14,20},{16,22},{... | collective-permute-start | bytes 276488 | tf_op jit(solution)/shard_map/ppermute | solution.py:404
  93.9 10.8 %collective-permute-start.10 = (bf16[16,2880]{1,0:T(8,128)(2,1)S(1)}, bf16[16,2880]{1,0:T(8,128)(2,1)S(1)}, u32[]{:S(2)}, u32[]{:S(2)}) collective-permute-start(bf16[16,2880]{1,0:T(8,128)(2,1)S(1)} %get-tuple-element.65), channel_id=1, source_target_pairs={{0,8},{2,10},{4,12},{6,14},{8,16},{10,18},{12,20},{14,22},{16,24},... | collective-permute-start | bytes 276488 | tf_op jit(solution)/shard_map/ppermute | solution.py:404
  96.5 14.1 %collective-permute-start.11 = (bf16[16,2880]{1,0:T(8,128)(2,1)S(1)}, bf16[16,2880]{1,0:T(8,128)(2,1)S(1)}, u32[]{:S(2)}, u32[]{:S(2)}) collective-permute-start(bf16[16,2880]{1,0:T(8,128)(2,1)S(1)} %get-tuple-element.66), channel_id=1, source_target_pairs={{0,10},{2,12},{4,14},{6,16},{8,18},{10,20},{12,22},{14,24},{16,26}... | collective-permute-start | bytes 276488 | tf_op jit(solution)/shard_map/ppermute | solution.py:404
  99.6 11.0 %collective-permute-start.12 = (bf16[16,2880]{1,0:T(8,128)(2,1)S(1)}, bf16[16,2880]{1,0:T(8,128)(2,1)S(1)}, u32[]{:S(2)}, u32[]{:S(2)}) collective-permute-start(bf16[16,2880]{1,0:T(8,128)(2,1)S(1)} %get-tuple-element.67), channel_id=1, source_target_pairs={{0,12},{2,14},{4,16},{6,18},{8,20},{10,22},{12,24},{14,26},{16,28}... | collective-permute-start | bytes 276488 | tf_op jit(solution)/shard_map/ppermute | solution.py:404
  102.5 10.0 %collective-permute-start.13 = (bf16[16,2880]{1,0:T(8,128)(2,1)S(1)}, bf16[16,2880]{1,0:T(8,128)(2,1)S(1)}, u32[]{:S(2)}, u32[]{:S(2)}) collective-permute-start(bf16[16,2880]{1,0:T(8,128)(2,1)S(1)} %get-tuple-element.68), channel_id=1, source_target_pairs={{0,14},{2,16},{4,18},{6,20},{8,22},{10,24},{12,26},{14,28},{16,30}... | collective-permute-start | bytes 276488 | tf_op jit(solution)/shard_map/ppermute | solution.py:404
  103.2 9.5 %collective-permute-start.14 = (bf16[16,2880]{1,0:T(8,128)(2,1)S(1)}, bf16[16,2880]{1,0:T(8,128)(2,1)S(1)}, u32[]{:S(2)}, u32[]{:S(2)}) collective-permute-start(bf16[16,2880]{1,0:T(8,128)(2,1)S(1)} %get-tuple-element.69), channel_id=1, source_target_pairs={{0,16},{2,18},{4,20},{6,22},{8,24},{10,26},{12,28},{14,30},{16,0},... | collective-permute-start | bytes 276488 | tf_op jit(solution)/shard_map/ppermute | solution.py:404
  104.7 11.9 %collective-permute-start.15 = (bf16[16,2880]{1,0:T(8,128)(2,1)S(1)}, bf16[16,2880]{1,0:T(8,128)(2,1)S(1)}, u32[]{:S(2)}, u32[]{:S(2)}) collective-permute-start(bf16[16,2880]{1,0:T(8,128)(2,1)S(1)} %get-tuple-element.70), channel_id=1, source_target_pairs={{0,18},{2,20},{4,22},{6,24},{8,26},{10,28},{12,30},{14,0},{16,2},{... | collective-permute-start | bytes 276488 | tf_op jit(solution)/shard_map/ppermute | solution.py:404
  110.5 6.8 %collective-permute-start.16 = (bf16[16,2880]{1,0:T(8,128)(2,1)S(1)}, bf16[16,2880]{1,0:T(8,128)(2,1)S(1)}, u32[]{:S(2)}, u32[]{:S(2)}) collective-permute-start(bf16[16,2880]{1,0:T(8,128)(2,1)S(1)} %get-tuple-element.71), channel_id=1, source_target_pairs={{0,20},{2,22},{4,24},{6,26},{8,28},{10,30},{12,0},{14,2},{16,4},{1... | collective-permute-start | bytes 276488 | tf_op jit(solution)/shard_map/ppermute | solution.py:404
  110.6 16.6 %collective-permute-start.17 = (bf16[16,2880]{1,0:T(8,128)(2,1)S(1)}, bf16[16,2880]{1,0:T(8,128)(2,1)S(1)}, u32[]{:S(2)}, u32[]{:S(2)}) collective-permute-start(bf16[16,2880]{1,0:T(8,128)(2,1)S(1)} %get-tuple-element.72), channel_id=1, source_target_pairs={{0,22},{2,24},{4,26},{6,28},{8,30},{10,0},{12,2},{14,4},{16,6},{18... | collective-permute-start | bytes 276488 | tf_op jit(solution)/shard_map/ppermute | solution.py:404
  112.4 14.7 %collective-permute-start.18 = (bf16[16,2880]{1,0:T(8,128)(2,1)S(1)}, bf16[16,2880]{1,0:T(8,128)(2,1)S(1)}, u32[]{:S(2)}, u32[]{:S(2)}) collective-permute-start(bf16[16,2880]{1,0:T(8,128)(2,1)S(1)} %get-tuple-element.73), channel_id=1, source_target_pairs={{0,24},{2,26},{4,28},{6,30},{8,0},{10,2},{12,4},{14,6},{16,8},{18,... | collective-permute-start | bytes 276488 | tf_op jit(solution)/shard_map/ppermute | solution.py:404
  112.6 14.5 %collective-permute-start.19 = (bf16[16,2880]{1,0:T(8,128)(2,1)S(1)}, bf16[16,2880]{1,0:T(8,128)(2,1)S(1)}, u32[]{:S(2)}, u32[]{:S(2)}) collective-permute-start(bf16[16,2880]{1,0:T(8,128)(2,1)S(1)} %get-tuple-element.74), channel_id=1, source_target_pairs={{0,26},{2,28},{4,30},{6,0},{8,2},{10,4},{12,6},{14,8},{16,10},{18,... | collective-permute-start | bytes 276488 | tf_op jit(solution)/shard_map/ppermute | solution.py:404
  116.6 10.6 %collective-permute-start.20 = (bf16[16,2880]{1,0:T(8,128)(2,1)S(1)}, bf16[16,2880]{1,0:T(8,128)(2,1)S(1)}, u32[]{:S(2)}, u32[]{:S(2)}) collective-permute-start(bf16[16,2880]{1,0:T(8,128)(2,1)S(1)} %get-tuple-element.75), channel_id=1, source_target_pairs={{0,28},{2,30},{4,0},{6,2},{8,4},{10,6},{12,8},{14,10},{16,12},{18,... | collective-permute-start | bytes 276488 | tf_op jit(solution)/shard_map/ppermute | solution.py:404
  117.3 9.9 %collective-permute-start.21 = (bf16[16,2880]{1,0:T(8,128)(2,1)S(1)}, bf16[16,2880]{1,0:T(8,128)(2,1)S(1)}, u32[]{:S(2)}, u32[]{:S(2)}) collective-permute-start(bf16[16,2880]{1,0:T(8,128)(2,1)S(1)} %get-tuple-element.76), channel_id=1, source_target_pairs={{0,30},{2,0},{4,2},{6,4},{8,6},{10,8},{12,10},{14,12},{16,14},{18,... | collective-permute-start | bytes 276488 | tf_op jit(solution)/shard_map/ppermute | solution.py:404
  127.2 35.3 %copy-start.9 = (f32[1,64,4]{1,2,0:T(4,128)S(1)}, f32[1,64,4]{1,2,0:T(4,128)}, u32[]{:S(2)}) copy-start(f32[1,64,4]{1,2,0:T(4,128)} %param.22) | copy-start | bytes 3076
  134.8 12.2 %collective-permute-start.22 = (bf16[64,1440]{1,0:T(8,128)(2,1)S(1)}, bf16[64,1440]{1,0:T(8,128)(2,1)S(1)}, u32[]{:S(2)}, u32[]{:S(2)}) collective-permute-start(bf16[64,1440]{1,0:T(8,128)(2,1)S(1)} %get-tuple-element.82), channel_id=1, source_target_pairs={{0,1},{1,0},{2,3},{3,2},{4,5},{5,4},{6,7},{7,6},{8,9},{9,8},{10,11... | collective-permute-start | bytes 552968 | tf_op jit(solution)/shard_map/ppermute | solution.py:404
  136.3 7.4 %collective-permute-start.23 = (bf16[48,1440]{1,0:T(8,128)(2,1)S(1)}, bf16[48,1440]{1,0:T(8,128)(2,1)S(1)}, u32[]{:S(2)}, u32[]{:S(2)}) collective-permute-start(bf16[48,1440]{1,0:T(8,128)(2,1)S(1)} %get-tuple-element.85), channel_id=1, source_target_pairs={{0,1},{1,0},{2,3},{3,2},{4,5},{5,4},{6,7},{7,6},{8,9},{9,8},{10,11... | collective-permute-start | bytes 414728 | tf_op jit(solution)/shard_map/ppermute | solution.py:404
  136.9 17.3 %collective-permute-start.27 = (bf16[64,1440]{1,0:T(8,128)(2,1)S(1)}, bf16[64,1440]{1,0:T(8,128)(2,1)S(1)}, u32[]{:S(2)}, u32[]{:S(2)}) collective-permute-start(bf16[64,1440]{1,0:T(8,128)(2,1)S(1)} %get-tuple-element.90), channel_id=1, source_target_pairs={{0,1},{1,0},{2,3},{3,2},{4,5},{5,4},{6,7},{7,6},{8,9},{9,8},{10,11... | collective-permute-start | bytes 552968 | tf_op jit(solution)/shard_map/ppermute | solution.py:404
  138.4 22.2 %collective-permute-start.32 = (bf16[80,1440]{1,0:T(8,128)(2,1)S(1)}, bf16[80,1440]{1,0:T(8,128)(2,1)S(1)}, u32[]{:S(2)}, u32[]{:S(2)}) collective-permute-start(bf16[80,1440]{1,0:T(8,128)(2,1)S(1)} %get-tuple-element.96), channel_id=1, source_target_pairs={{0,1},{1,0},{2,3},{3,2},{4,5},{5,4},{6,7},{7,6},{8,9},{9,8},{10,11... | collective-permute-start | bytes 691208 | tf_op jit(solution)/shard_map/ppermute | solution.py:404
  143.7 5.7 %collective-permute-start.24 = (bf16[16,1440]{1,0:T(8,128)(2,1)S(1)}, bf16[16,1440]{1,0:T(8,128)(2,1)S(1)}, u32[]{:S(2)}, u32[]{:S(2)}) collective-permute-start(bf16[16,1440]{1,0:T(8,128)(2,1)S(1)} %get-tuple-element.86), channel_id=1, source_target_pairs={{0,30},{2,0},{4,2},{6,4},{8,6},{10,8},{12,10},{14,12},{16,14},{18,... | collective-permute-start | bytes 138248 | tf_op jit(solution)/shard_map/ppermute | solution.py:404
  147.0 7.3 %collective-permute-start.25 = (bf16[16,1440]{1,0:T(8,128)(2,1)S(1)}, bf16[16,1440]{1,0:T(8,128)(2,1)S(1)}, u32[]{:S(2)}, u32[]{:S(2)}) collective-permute-start(bf16[16,1440]{1,0:T(8,128)(2,1)S(1)} %get-tuple-element.87), channel_id=1, source_target_pairs={{0,28},{2,30},{4,0},{6,2},{8,4},{10,6},{12,8},{14,10},{16,12},{18,... | collective-permute-start | bytes 138248 | tf_op jit(solution)/shard_map/ppermute | solution.py:404
  147.0 7.9 %collective-permute-start.26 = (bf16[16,1440]{1,0:T(8,128)(2,1)S(1)}, bf16[16,1440]{1,0:T(8,128)(2,1)S(1)}, u32[]{:S(2)}, u32[]{:S(2)}) collective-permute-start(bf16[16,1440]{1,0:T(8,128)(2,1)S(1)} %get-tuple-element.88), channel_id=1, source_target_pairs={{0,26},{2,28},{4,30},{6,0},{8,2},{10,4},{12,6},{14,8},{16,10},{18,... | collective-permute-start | bytes 138248 | tf_op jit(solution)/shard_map/ppermute | solution.py:404
  149.4 8.4 %collective-permute-start.38 = (bf16[16,1440]{1,0:T(8,128)(2,1)S(1)}, bf16[16,1440]{1,0:T(8,128)(2,1)S(1)}, u32[]{:S(2)}, u32[]{:S(2)}) collective-permute-start(bf16[16,1440]{1,0:T(8,128)(2,1)S(1)} %get-tuple-element.102), channel_id=1, source_target_pairs={{0,6},{2,8},{4,10},{6,12},{8,14},{10,16},{12,18},{14,20},{16,22},{... | collective-permute-start | bytes 138248 | tf_op jit(solution)/shard_map/ppermute | solution.py:404
  154.2 6.3 %collective-permute-start.39 = (bf16[16,1440]{1,0:T(8,128)(2,1)S(1)}, bf16[16,1440]{1,0:T(8,128)(2,1)S(1)}, u32[]{:S(2)}, u32[]{:S(2)}) collective-permute-start(bf16[16,1440]{1,0:T(8,128)(2,1)S(1)} %get-tuple-element.103), channel_id=1, source_target_pairs={{0,4},{2,6},{4,8},{6,10},{8,12},{10,14},{12,16},{14,18},{16,20},{1... | collective-permute-start | bytes 138248 | tf_op jit(solution)/shard_map/ppermute | solution.py:404
  154.3 8.4 %collective-permute-start.40 = (bf16[16,1440]{1,0:T(8,128)(2,1)S(1)}, bf16[16,1440]{1,0:T(8,128)(2,1)S(1)}, u32[]{:S(2)}, u32[]{:S(2)}) collective-permute-start(bf16[16,1440]{1,0:T(8,128)(2,1)S(1)} %get-tuple-element.104), channel_id=1, source_target_pairs={{0,2},{2,4},{4,6},{6,8},{8,10},{10,12},{12,14},{14,16},{16,18},{18... | collective-permute-start | bytes 138248 | tf_op jit(solution)/shard_map/ppermute | solution.py:404
  154.9 10.1 %collective-permute-start.28 = (bf16[16,1440]{1,0:T(8,128)(2,1)S(1)}, bf16[16,1440]{1,0:T(8,128)(2,1)S(1)}, u32[]{:S(2)}, u32[]{:S(2)}) collective-permute-start(bf16[16,1440]{1,0:T(8,128)(2,1)S(1)} %get-tuple-element.91), channel_id=1, source_target_pairs={{0,24},{2,26},{4,28},{6,30},{8,0},{10,2},{12,4},{14,6},{16,8},{18,... | collective-permute-start | bytes 138248 | tf_op jit(solution)/shard_map/ppermute | solution.py:404
  157.8 8.1 %collective-permute-start.29 = (bf16[16,1440]{1,0:T(8,128)(2,1)S(1)}, bf16[16,1440]{1,0:T(8,128)(2,1)S(1)}, u32[]{:S(2)}, u32[]{:S(2)}) collective-permute-start(bf16[16,1440]{1,0:T(8,128)(2,1)S(1)} %get-tuple-element.92), channel_id=1, source_target_pairs={{0,22},{2,24},{4,26},{6,28},{8,30},{10,0},{12,2},{14,4},{16,6},{18... | collective-permute-start | bytes 138248 | tf_op jit(solution)/shard_map/ppermute | solution.py:404
  160.5 6.8 %collective-permute-start.30 = (bf16[16,1440]{1,0:T(8,128)(2,1)S(1)}, bf16[16,1440]{1,0:T(8,128)(2,1)S(1)}, u32[]{:S(2)}, u32[]{:S(2)}) collective-permute-start(bf16[16,1440]{1,0:T(8,128)(2,1)S(1)} %get-tuple-element.93), channel_id=1, source_target_pairs={{0,20},{2,22},{4,24},{6,26},{8,28},{10,30},{12,0},{14,2},{16,4},{1... | collective-permute-start | bytes 138248 | tf_op jit(solution)/shard_map/ppermute | solution.py:404
  160.6 7.7 %collective-permute-start.31 = (bf16[16,1440]{1,0:T(8,128)(2,1)S(1)}, bf16[16,1440]{1,0:T(8,128)(2,1)S(1)}, u32[]{:S(2)}, u32[]{:S(2)}) collective-permute-start(bf16[16,1440]{1,0:T(8,128)(2,1)S(1)} %get-tuple-element.94), channel_id=1, source_target_pairs={{0,18},{2,20},{4,22},{6,24},{8,26},{10,28},{12,30},{14,0},{16,2},{... | collective-permute-start | bytes 138248 | tf_op jit(solution)/shard_map/ppermute | solution.py:404
  162.7 6.4 %collective-permute-start.33 = (bf16[16,1440]{1,0:T(8,128)(2,1)S(1)}, bf16[16,1440]{1,0:T(8,128)(2,1)S(1)}, u32[]{:S(2)}, u32[]{:S(2)}) collective-permute-start(bf16[16,1440]{1,0:T(8,128)(2,1)S(1)} %get-tuple-element.97), channel_id=1, source_target_pairs={{0,16},{2,18},{4,20},{6,22},{8,24},{10,26},{12,28},{14,30},{16,0},... | collective-permute-start | bytes 138248 | tf_op jit(solution)/shard_map/ppermute | solution.py:404
  165.0 5.0 %collective-permute-start.34 = (bf16[16,1440]{1,0:T(8,128)(2,1)S(1)}, bf16[16,1440]{1,0:T(8,128)(2,1)S(1)}, u32[]{:S(2)}, u32[]{:S(2)}) collective-permute-start(bf16[16,1440]{1,0:T(8,128)(2,1)S(1)} %get-tuple-element.98), channel_id=1, source_target_pairs={{0,14},{2,16},{4,18},{6,20},{8,22},{10,24},{12,26},{14,28},{16,30}... | collective-permute-start | bytes 138248 | tf_op jit(solution)/shard_map/ppermute | solution.py:404
  165.9 6.9 %collective-permute-start.35 = (bf16[16,1440]{1,0:T(8,128)(2,1)S(1)}, bf16[16,1440]{1,0:T(8,128)(2,1)S(1)}, u32[]{:S(2)}, u32[]{:S(2)}) collective-permute-start(bf16[16,1440]{1,0:T(8,128)(2,1)S(1)} %get-tuple-element.99), channel_id=1, source_target_pairs={{0,12},{2,14},{4,16},{6,18},{8,20},{10,22},{12,24},{14,26},{16,28}... | collective-permute-start | bytes 138248 | tf_op jit(solution)/shard_map/ppermute | solution.py:404
  167.3 6.8 %collective-permute-start.36 = (bf16[16,1440]{1,0:T(8,128)(2,1)S(1)}, bf16[16,1440]{1,0:T(8,128)(2,1)S(1)}, u32[]{:S(2)}, u32[]{:S(2)}) collective-permute-start(bf16[16,1440]{1,0:T(8,128)(2,1)S(1)} %get-tuple-element.100), channel_id=1, source_target_pairs={{0,10},{2,12},{4,14},{6,16},{8,18},{10,20},{12,22},{14,24},{16,26}... | collective-permute-start | bytes 138248 | tf_op jit(solution)/shard_map/ppermute | solution.py:404
  168.2 5.9 %collective-permute-start.37 = (bf16[16,1440]{1,0:T(8,128)(2,1)S(1)}, bf16[16,1440]{1,0:T(8,128)(2,1)S(1)}, u32[]{:S(2)}, u32[]{:S(2)}) collective-permute-start(bf16[16,1440]{1,0:T(8,128)(2,1)S(1)} %get-tuple-element.101), channel_id=1, source_target_pairs={{0,8},{2,10},{4,12},{6,14},{8,16},{10,18},{12,20},{14,22},{16,24},... | collective-permute-start | bytes 138248 | tf_op jit(solution)/shard_map/ppermute | solution.py:404
  (4 other events, 25.0 us)
